TPU v7x, 32 devices: a 4x4x1 block of a 4x4x8 slice. The times are simulated.
32 devices in a mesh: dp: 1 (over z), dpa: 32 (over y, x, core).
Axes of the slice: x: 4, y: 4, z: 1, core: 2. Of those that a mesh axis runs over, the one named last changes fastest.
The devices are a block of a 4x4x8 slice.
Arguments:
- x: bfloat16 [32, 1, 512, 2048], P(('dp', 'dpa'))
- chunk_len: int32 [32, 1], P(('dp', 'dpa'))
- ctx_len: int32 [32, 1], P(('dp', 'dpa'))
- lat_cache: bfloat16 [32, 1, 1024, 512], P(('dp', 'dpa'))
- rope_cache: bfloat16 [32, 1, 1024, 64], P(('dp', 'dpa'))
- topk_idx: int32 [32, 1, 512, 6], P(('dp', 'dpa'))
- g_attn: bfloat16 [2048], replicated
- w_q: bfloat16 [2048, 16, 192], replicated
- w_dkv: bfloat16 [2048, 512], replicated
- g_kv: bfloat16 [512], replicated
- w_kr: bfloat16 [2048, 64], replicated
- w_uk: bfloat16 [512, 16, 128], replicated
- w_uv: bfloat16 [512, 16, 128], replicated
- w_o: bfloat16 [16, 128, 2048], replicated
- g_ffn: bfloat16 [2048], replicated
- w_router: bfloat16 [2048, 64], replicated
- w_sh_gate: bfloat16 [2048, 2816], replicated
- w_sh_up: bfloat16 [2048, 2816], replicated
- w_sh_down: bfloat16 [2816, 2048], replicated
- w_exp_gate: bfloat16 [64, 2048, 1408], P('dpa')
- w_exp_up: bfloat16 [64, 2048, 1408], P('dpa')
- w_exp_down: bfloat16 [64, 1408, 2048], P('dpa')
Outputs:
- output 1: bfloat16 [32, 1, 512, 2048], P(('dp', 'dpa'))
- output 2: bfloat16 [32, 1, 1024, 512], P(('dp', 'dpa'))
- output 3: bfloat16 [32, 1, 1024, 64], P(('dp', 'dpa'))
All inputs are finite; a program needn't handle non-finite values.
Results may differ from a plain program's by a relative error of at most 0.0196077.
Values are sent between devices in bfloat16 or wider.
A program may use at most 768 MiB of HBM per device.

v0:
```python
import jax
import jax.numpy as jnp
from jax import lax
from jax.sharding import PartitionSpec as P

EPS = 1e-6
THETA = 10000.0


def rms_norm(vals, gain):
    vals_f32 = vals.astype(jnp.float32)
    inv_rms = lax.rsqrt(jnp.mean(vals_f32 * vals_f32, axis=-1, keepdims=True) + EPS)
    return (vals_f32 * inv_rms * gain.astype(jnp.float32)).astype(jnp.bfloat16)


def rope_tables(positions, half):
    inv_freq = THETA ** (-2.0 * jnp.arange(half, dtype=jnp.float32) / (2 * half))
    angle = positions.astype(jnp.float32)[..., None] * inv_freq
    return jnp.cos(angle), jnp.sin(angle)


def rotate(vals, cos_tab, sin_tab):
    half = cos_tab.shape[-1]
    first = vals[..., :half]
    second = vals[..., half:]
    return jnp.concatenate([first * cos_tab - second * sin_tab, second * cos_tab + first * sin_tab], axis=-1)


def write_window(cache_row, new_rows, start, keep):
    old_rows = lax.dynamic_slice_in_dim(cache_row, start, new_rows.shape[0], axis=0)
    merged = jnp.where(keep[:, None], new_rows, old_rows)
    return lax.dynamic_update_slice_in_dim(cache_row, merged, start, axis=0)


def attention_block(x_in, chunk_len, ctx_len, lat_cache, rope_cache, g_attn, w_q, w_dkv, g_kv, w_kr, w_uk, w_uv, w_o):
    chunk = x_in.shape[2]
    ctx_max = lat_cache.shape[2]
    rope_dim = w_kr.shape[1]
    nope_dim = w_q.shape[2] - rope_dim
    scale = w_q.shape[2] ** -0.5
    normed = rms_norm(x_in, g_attn)
    q_full = jnp.einsum('brcd,dhq->brchq', normed, w_q, preferred_element_type=jnp.float32).astype(jnp.bfloat16)
    positions = ctx_len[:, :, None] + jnp.arange(chunk)
    cos_tab, sin_tab = rope_tables(positions, rope_dim // 2)
    q_rope = rotate(q_full[..., nope_dim:].astype(jnp.float32), cos_tab[..., None, :], sin_tab[..., None, :]).astype(jnp.bfloat16)
    q_lat = jnp.einsum('brchn,khn->brchk', q_full[..., :nope_dim], w_uk, preferred_element_type=jnp.float32).astype(jnp.bfloat16)
    lat_new = rms_norm(jnp.einsum('brcd,dk->brck', normed, w_dkv, preferred_element_type=jnp.float32), g_kv)
    rope_new = rotate(jnp.einsum('brcd,dp->brcp', normed, w_kr, preferred_element_type=jnp.float32), cos_tab, sin_tab).astype(jnp.bfloat16)
    keep = jnp.arange(chunk) < chunk_len[:, :, None]
    writer = jax.vmap(jax.vmap(write_window))
    lat_upd = writer(lat_cache, lat_new, ctx_len, keep)
    rope_upd = writer(rope_cache, rope_new, ctx_len, keep)
    key_pos = jnp.arange(ctx_max)

    def one_request(index):
        q_lat_req = lax.dynamic_index_in_dim(q_lat, index, axis=1, keepdims=False)
        q_rope_req = lax.dynamic_index_in_dim(q_rope, index, axis=1, keepdims=False)
        lat_req = lax.dynamic_index_in_dim(lat_upd, index, axis=1, keepdims=False)
        rope_req = lax.dynamic_index_in_dim(rope_upd, index, axis=1, keepdims=False)
        pos_req = lax.dynamic_index_in_dim(positions, index, axis=1, keepdims=False)
        scores = (jnp.einsum('bchk,blk->bchl', q_lat_req, lat_req, preferred_element_type=jnp.float32) + jnp.einsum('bchp,blp->bchl', q_rope_req, rope_req, preferred_element_type=jnp.float32)) * scale
        visible = key_pos[None, None, None, :] <= pos_req[:, :, None, None]
        scores = jnp.where(visible, scores, -1e30)
        attn_prob = jax.nn.softmax(scores, axis=-1).astype(jnp.bfloat16)
        return jnp.einsum('bchl,blk->bchk', attn_prob, lat_req, preferred_element_type=jnp.float32).astype(jnp.bfloat16)

    out_lat = lax.map(one_request, jnp.arange(x_in.shape[1]))
    out_head = jnp.einsum('rbchk,khv->brchv', out_lat, w_uv, preferred_element_type=jnp.float32).astype(jnp.bfloat16)
    attn_out = jnp.einsum('brchv,hvd->brcd', out_head, w_o, preferred_element_type=jnp.float32).astype(jnp.bfloat16)
    hidden = (x_in.astype(jnp.float32) + attn_out.astype(jnp.float32)).astype(jnp.bfloat16)
    return hidden, lat_upd, rope_upd


def router_and_shared(hidden_rows, g_ffn, w_router, w_sh_gate, w_sh_up, w_sh_down):
    normed = rms_norm(hidden_rows, g_ffn)
    route_prob = jax.nn.softmax(jnp.dot(normed, w_router, preferred_element_type=jnp.float32), axis=-1)
    shared_act = (jax.nn.silu(jnp.dot(normed, w_sh_gate, preferred_element_type=jnp.float32)) * jnp.dot(normed, w_sh_up, preferred_element_type=jnp.float32)).astype(jnp.bfloat16)
    shared_out = jnp.dot(shared_act, w_sh_down, preferred_element_type=jnp.float32)
    return normed, route_prob, shared_out


def expert_ffn(sorted_rows, sizes, w_exp_gate, w_exp_up, w_exp_down):
    gate_part = lax.ragged_dot(sorted_rows, w_exp_gate, sizes, preferred_element_type=jnp.float32)
    up_part = lax.ragged_dot(sorted_rows, w_exp_up, sizes, preferred_element_type=jnp.float32)
    act = (jax.nn.silu(gate_part) * up_part).astype(jnp.bfloat16)
    return lax.ragged_dot(act, w_exp_down, sizes, preferred_element_type=jnp.float32).astype(jnp.bfloat16)


def solution(mesh):
    group = mesh.shape['dpa']
    tok_spec = P(('dp', 'dpa'))
    whole = P()
    exp_spec = P('dpa')

    def device_step(x_in, chunk_len, ctx_len, lat_cache, rope_cache, topk_idx, g_attn, w_q, w_dkv, g_kv, w_kr, w_uk, w_uv, w_o, g_ffn, w_router, w_sh_gate, w_sh_up, w_sh_down, w_exp_gate, w_exp_up, w_exp_down):
        hidden, lat_upd, rope_upd = attention_block(x_in, chunk_len, ctx_len, lat_cache, rope_cache, g_attn, w_q, w_dkv, g_kv, w_kr, w_uk, w_uv, w_o)
        chunk = hidden.shape[2]
        width = hidden.shape[3]
        tokens = hidden.shape[1] * chunk
        top_k = topk_idx.shape[-1]
        local_exp = w_exp_gate.shape[0]
        capacity = tokens * top_k // group
        flat_h = hidden.reshape(tokens, width)
        normed, route_prob, shared_out = router_and_shared(flat_h, g_ffn, w_router, w_sh_gate, w_sh_up, w_sh_down)
        valid = (jnp.arange(chunk)[None, :] < chunk_len[0][:, None]).reshape(tokens)
        choice = topk_idx.reshape(tokens, top_k)
        gates = jnp.take_along_axis(route_prob, choice, axis=1)
        flat_choice = choice.reshape(tokens * top_k)
        target = flat_choice // local_exp
        hits = (target[:, None] == jnp.arange(group)[None, :]).astype(jnp.int32)
        rank_in = jnp.sum(jnp.cumsum(hits, axis=0) * hits, axis=1) - 1
        slot = target * capacity + rank_in
        pair_of_slot = jnp.argsort(slot)
        pair_valid = jnp.repeat(valid, top_k)
        expert_key = jnp.where(pair_valid, flat_choice % local_exp, local_exp).astype(jnp.int32)
        send_rows = normed[pair_of_slot // top_k]
        send_key = expert_key[pair_of_slot]
        recv_rows = lax.all_to_all(send_rows, 'dpa', 0, 0, tiled=True)
        recv_key = lax.all_to_all(send_key, 'dpa', 0, 0, tiled=True)
        order = jnp.argsort(recv_key, stable=True)
        sizes = jnp.bincount(recv_key, length=local_exp + 1)[:local_exp].astype(jnp.int32)
        sorted_out = expert_ffn(recv_rows[order], sizes, w_exp_gate, w_exp_up, w_exp_down)
        expert_rows = sorted_out[jnp.argsort(order)]
        back_rows = lax.all_to_all(expert_rows, 'dpa', 0, 0, tiled=True)
        pair_out = back_rows[slot].reshape(tokens, top_k, width)
        routed = jnp.sum(gates[:, :, None] * pair_out.astype(jnp.float32), axis=1)
        total = flat_h.astype(jnp.float32) + shared_out + routed
        result = jnp.where(valid[:, None], total, 0.0).astype(jnp.bfloat16)
        return result.reshape(hidden.shape), lat_upd, rope_upd

    return jax.shard_map(device_step, mesh=mesh, in_specs=(tok_spec,) * 6 + (whole,) * 13 + (exp_spec,) * 3, out_specs=(tok_spec, tok_spec, tok_spec), check_vma=False)
```

profile of v0, /device:TPU:103, one launch (start us, length us, event | category | flops | bytes accessed | tf_op | source)
XLA Modules:
  0.0 851.3 jit_solution(4851570692096099610)
XLA Ops:
  6.2 17.9 %reduce-window.6 = s32[32,24,128]{2,1,0:T(8,128)} reduce-window(s32[32,24,128]{2,1,0:T(8,128)} %fusion.43, s32[]{:T(128)} %constant.174.clone.1), window={size=1x1x128 pad=0_0x0_0x127_0}, to_apply=%region_8.9 | reduce-window | flops 12484608 | bytes 786436 | tf_op jit(solution)/shard_map/reduce-window
  24.1 1.9 slice.150
  26.0 1.9 copy.60
  29.3 1.9 broadcast_add_fusion
  36.6 5.8 sort.48
  42.9 17.4 %gather_fusion.1 = s32[3072]{0:T(1024)S(1)} fusion(s32[3072]{0:T(1024)S(1)} %get-tuple-element.101, s32[3072]{0:T(1024)S(1)} %get-tuple-element.103), kind=kCustom, calls=%fused_computation.1 | custom fusion | bytes 36864 | tf_op jit(solution)/shard_map/gather | solution.py:117
  61.0 8.0 all-to-all-start.1
  69.1 2.1 fusion.9
  71.2 10.2 %fusion.85 = f32[512,3072]{0,1:S(1)} fusion(bf16[2048,3072]{0,1:T(8,128)(2,1)} %bitcast.155, bf16[1,1,512,2048]{3,2,1,0:T(8,128)(2,1)} %param.26, f32[2048]{0:T(1024)S(1)} %convert_element_type.134, f32[512]{0:T(512)S(1)} %add_rsqrt_fusion.2), kind=kOutput, calls=%fused_computation.155 | convolution fusion | flops 6446645248 | bytes 20981760
  81.4 2.1 convert_bitcast_fusion
  85.5 2.4 constant_dynamic-slice_fusion
  87.9 2.0 copy.61
  89.9 4.6 multiply_reduce_fusion.1
  94.5 2.1 copy.47
  96.6 2.0 and_reduce_fusion
  98.6 3.1 fusion.38
  101.7 2.0 copy.49
  103.7 4.8 scatter.6
  109.9 2.8 slice_convert_fusion
  112.7 2.4 convolution_bitcast_fusion
  115.8 2.0 fusion.57
  119.2 18.9 %fusion.2 = f32[512,16,1024]{2,0,1:T(8,128)} fusion(bf16[1,1,512,16,192]{2,4,3,1,0:T(8,128)(2,1)} %convert_bitcast_fusion, bf16[512,16,128]{2,1,0:T(8,128)(2,1)S(1)} %copy-done, bf16[1,1,1024,512]{3,2,1,0:T(8,128)(2,1)} %copy-done.6), kind=kOutput, calls=%fused_computation.14 | convolution fusion | flops 9667870720 | bytes 38797312 | tf_op jit(solution)/shard_map/while/body/eval_jaxpr/bchk,blk->bchl/dot_general | solution.py:61
  138.1 1.9 fusion.39
  140.0 16.5 %fusion.89 = f32[512,16]{0,1:T(8,128)S(1)} fusion(f32[512,16,1024]{2,0,1:T(8,128)} %fusion.2, pred[512,1024]{1,0:T(8,128)(4,1)S(1)} %iota_compare_fusion, bf16[512,16,32]{0,2,1:T(8,128)(2,1)S(1)} %get-tuple-element.94, bf16[512,16,32]{0,2,1:T(8,128)(2,1)S(1)} %get-tuple-element.93, bf16[1,1,1024,64]{2,3,1,0:T(8,128)(2,1)S(1)} %scatter.9), kind=kOutput, calls=%fused_computation.158 | convolution fusion | flops 1117783040 | bytes 35291136 | tf_op jit(solution)/shard_map/while/body/eval_jaxpr/sub | solution.py:64
  156.6 21.7 %multiply_select_fusion = f32[512,16,1024]{2,0,1:T(8,128)} fusion(f32[512,16,1024]{2,0,1:T(8,128)} %fusion.2, pred[512,1024]{1,0:T(8,128)(4,1)S(1)} %iota_compare_fusion, bf16[512,16,32]{0,2,1:T(8,128)(2,1)S(1)} %get-tuple-element.94, bf16[512,16,32]{0,2,1:T(8,128)(2,1)S(1)} %get-tuple-element.93, bf16[1,1,1024,64]{2,3,1,0:T(8,128)(2,1)S(1)} %scatter.9), kind=kOutput, calls=%fused_computation.11 | convolution fusion | flops 1101004800 | bytes 68812800 | tf_op jit(solution)/shard_map/while/body/eval_jaxpr/bchp,blp->bchl/dot_general | solution.py:61
  178.3 35.7 %fusion.4 = bf16[16,512,128]{2,1,0:T(8,128)(2,1)} fusion(f32[512,16]{0,1:T(8,128)S(1)} %fusion.89, bf16[512,16,128]{2,1,0:T(8,128)(2,1)} %param.38, f32[512,16,1024]{2,0,1:T(8,128)} %multiply_select_fusion, bf16[1,1,1024,512]{3,2,1,0:T(8,128)(2,1)S(1)} %copy-done.7), kind=kOutput, calls=%fused_computation.16 | convolution fusion | flops 9693045760 | bytes 38830080 | tf_op jit(solution)/shard_map/rbchk,khv->brchv/dot_general | solution.py:68
  213.9 8.1 fusion.13
  224.0 16.0 %gather_fusion = bf16[3072,2048]{1,0:T(8,128)(2,1)} fusion(bf16[512,2048]{1,0:T(8,128)(2,1)S(1)} %fusion.15, s32[3072]{0:T(1024)S(1)} %copy-done.11), kind=kCustom, calls=%fused_computation | custom fusion | bytes 25178112 | tf_op jit(solution)/shard_map/gather | solution.py:116
  239.9 6.3 all-to-all-start
  248.2 22.3 %scatter_custom_fusion = s32[3]{0:T(128)} fusion(s32[3072]{0:T(1024)S(1)} %reshape.852, s32[3072]{0:T(1024)S(1)} %ne.62, s32[]{:T(128)} %constant.174.clone.1), kind=kCustom, calls=%fused_computation.146 | custom fusion | flops 3072 | bytes 16 | tf_op jit(solution)/shard_map/scatter-add | solution.py:121
  272.1 5.8 sort.49
  277.9 5.8 sort.50
  283.6 134.5 %all-to-all-done = bf16[32,96,2048]{2,1,0:T(8,128)(2,1)} async-done(((bf16[32,96,2048]{2,1,0:T(8,128)(2,1)}), bf16[32,96,2048]{2,1,0:T(8,128)(2,1)}, u32[]{:S(2)}, u32[]{:S(2)}) %all-to-all-start) | async-done | bytes 12582944 | tf_op jit(solution)/shard_map/all_to_all | solution.py:118
  418.2 30.0 %gather_fusion.2 = bf16[3072,2048]{1,0:T(8,128)(2,1)} fusion(bf16[3072,2048]{1,0:T(8,128)(2,1)} %bitcast.41, s32[3072]{0:T(1024)S(1)} %fusion.62), kind=kCustom, calls=%fused_computation.2 | custom fusion | bytes 25178112 | tf_op jit(solution)/shard_map/gather | solution.py:122
  448.2 23.7 %ragged-dot-none.1 = f32[3072,1408]{1,0:T(8,128)} custom-call(s32[1]{0:T(128)} %get-tuple-element.79, s32[3]{0:T(128)} %get-tuple-element.80, s32[13]{0:T(128)} %get-tuple-element.81, s32[13]{0:T(128)} %get-tuple-element.82, s32[1]{0:T(128)} %get-tuple-element.79, bf16[3072,2048]{1,0:T(8,128)(2,1)} %gather_fusion.2, bf16[2,2048,1408]{2,1,0:T(8,128)(2,1)} %param.46), custom_call_target="tpu_custom_call" | custom-call | flops 17716740096 | bytes 41418760 | tf_op jit(solution)/shard_map/ragged_dot_general/ragged-dot-none
  471.9 23.7 %ragged-dot-none.2 = f32[3072,1408]{1,0:T(8,128)} custom-call(s32[1]{0:T(128)} %get-tuple-element.79, s32[3]{0:T(128)} %get-tuple-element.80, s32[13]{0:T(128)} %get-tuple-element.81, s32[13]{0:T(128)} %get-tuple-element.82, s32[1]{0:T(128)} %get-tuple-element.79, bf16[3072,2048]{1,0:T(8,128)(2,1)} %gather_fusion.2, bf16[2,2048,1408]{2,1,0:T(8,128)(2,1)} %param.45), custom_call_target="tpu_custom_call" | custom-call | flops 17716740096 | bytes 41418760 | tf_op jit(solution)/shard_map/ragged_dot_general/ragged-dot-none
  495.6 15.5 %multiply_convert_fusion = bf16[3072,1408]{1,0:T(8,128)(2,1)} fusion(f32[3072,1408]{1,0:T(8,128)} %ragged-dot-none.1, f32[3072,1408]{1,0:T(8,128)} %ragged-dot-none.2), kind=kLoop, calls=%fused_computation.12 | loop fusion | flops 25952256 | bytes 43253760 | tf_op jit(solution)/shard_map/convert_element_type | solution.py:85
  511.1 24.2 %ragged-dot-none = f32[3072,2048]{1,0:T(8,128)} custom-call(s32[1]{0:T(128)} %get-tuple-element.79, s32[3]{0:T(128)} %get-tuple-element.80, s32[13]{0:T(128)} %get-tuple-element.81, s32[13]{0:T(128)} %get-tuple-element.82, s32[1]{0:T(128)} %get-tuple-element.79, bf16[3072,1408]{1,0:T(8,128)(2,1)} %multiply_convert_fusion, bf16[2,1408,2048]{2,1,0:T(8,128)(2,1)} %param.47), custom_call_target="tpu_custom_call" | custom-call | flops 17716740096 | bytes 45350920 | tf_op jit(solution)/shard_map/ragged_dot_general/ragged-dot-none
  535.3 13.4 %convert_element_type.163 = bf16[3072,2048]{1,0:T(8,128)(2,1)} convert(f32[3072,2048]{1,0:T(8,128)} %ragged-dot-none) | non-fusion elementwise | flops 6291456 | bytes 37748736 | tf_op jit(solution)/shard_map/convert_element_type | solution.py:86
  548.7 30.0 %gather_fusion.3 = bf16[3072,2048]{1,0:T(8,128)(2,1)} fusion(bf16[3072,2048]{1,0:T(8,128)(2,1)} %convert_element_type.163, s32[3072]{0:T(1024)S(1)} %fusion.63), kind=kCustom, calls=%fused_computation.3 | custom fusion | bytes 25178112 | tf_op jit(solution)/shard_map/gather | solution.py:123
  578.7 4.2 all-to-all-start.2
  584.3 24.9 %gather_fusion.5 = f32[3072]{0:T(1024)S(1)} fusion(f32[512,64]{0,1:T(8,128)S(1)} %fusion.47, s32[3072]{0:T(1024)S(1)} %reshape.844), kind=kCustom, calls=%fused_computation.5 | custom fusion | bytes 49152 | tf_op jit(solution)/shard_map/jit(take_along_axis)/gather | solution.py:107
  609.6 12.5 %fusion.95 = f32[512,2816]{1,0:T(8,128)} fusion(bf16[512,2048]{1,0:T(8,128)(2,1)} %copy-done.2, bf16[2048,2816]{1,0:T(8,128)(2,1)} %param.42), kind=kOutput, calls=%fused_computation.160 | convolution fusion | flops 5905580032 | bytes 19398656 | tf_op jit(solution)/shard_map/dot_general | solution.py:77
  622.1 132.0 %all-to-all-done.2 = bf16[32,96,2048]{2,1,0:T(8,128)(2,1)} async-done(((bf16[32,96,2048]{2,1,0:T(8,128)(2,1)}), bf16[32,96,2048]{2,1,0:T(8,128)(2,1)}, u32[]{:S(2)}, u32[]{:S(2)}) %all-to-all-start.2) | async-done | bytes 12582944 | tf_op jit(solution)/shard_map/all_to_all | solution.py:124
  754.1 30.0 %gather_fusion.4 = bf16[3072,2048]{1,0:T(8,128)(2,1)} fusion(bf16[3072,2048]{1,0:T(8,128)(2,1)} %bitcast.43, s32[3072]{0:T(1024)S(1)} %broadcast_clamp_fusion), kind=kCustom, calls=%fused_computation.4 | custom fusion | bytes 25178112 | tf_op jit(solution)/shard_map/gather | solution.py:125
  784.1 22.1 %reshape.801 = f32[512,6,2048]{2,1,0:T(8,128)} reshape(bf16[3072,2048]{1,0:T(8,128)(2,1)} %gather_fusion.4) | data formatting | bytes 37748736 | tf_op jit(solution)/shard_map/convert_element_type | solution.py:126
  806.2 19.3 %multiply_reduce_fusion = f32[512,2048]{1,0:T(8,128)} fusion(f32[512,6,2048]{2,1,0:T(8,128)} %reshape.801, f32[512,6]{1,0:T(8,128)S(1)} %and_select_fusion), kind=kLoop, calls=%fused_computation.8 | loop fusion | flops 11534336 | bytes 29372416 | tf_op jit(solution)/shard_map/reduce_sum | solution.py:126
  825.5 25.4 %fusion.20 = bf16[1,1,512,2048]{3,2,1,0:T(8,128)(2,1)} fusion(f32[512,2048]{1,0:T(8,128)} %multiply_reduce_fusion, bf16[2816,2048]{1,0:T(8,128)(2,1)} %param.44, bf16[512,2048]{1,0:T(8,128)(2,1)} %copy-done.8, pred[512]{0:T(512)(128)(4,1)S(1)} %copy-done.16, f32[512,2816]{1,0:T(8,128)} %fusion.95, bf16[512,2048]{1,0:T(8,128)(2,1)} %copy-done.2, ...), kind=kOutput, calls=%fused_computation.40 | convolution fusion | flops 11825053696 | bytes 39322112 | tf_op jit(solution)/shard_map/dot_general | solution.py:78
  (102 shorter events, 24.9 us)
Async XLA Ops:
  0.6 118.5 %copy-start = (bf16[512,16,128]{2,1,0:T(8,128)(2,1)S(1)}, bf16[512,16,128]{2,1,0:T(8,128)(2,1)}, u32[]{:S(2)}) copy-start(bf16[512,16,128]{2,1,0:T(8,128)(2,1)} %param.37) | copy-start | bytes 6291460
  3.8 31.1 %copy-start.4 = (s32[1,1,512,6]{3,2,1,0:T(8,128)}, s32[1,1,512,6]{3,2,1,0:T(8,128)S(1)}, u32[]{:S(2)}) copy-start(s32[1,1,512,6]{3,2,1,0:T(8,128)S(1)} %copy.51) | copy-start | bytes 36868
  32.5 0.5 copy-start.14
  42.9 26.1 %copy-start.17 = (bf16[2048]{0:T(1024)(128)(2,1)S(1)}, bf16[2048]{0:T(1024)(128)(2,1)}, u32[]{:S(2)}) copy-start(bf16[2048]{0:T(1024)(128)(2,1)} %param.32) | copy-start | bytes 12292
  61.0 178.9 %all-to-all-start.1 = ((s32[32,96,1]{1,2,0:T(1,128)}), s32[32,96,1]{1,2,0:T(1,128)}, u32[]{:S(2)}, u32[]{:S(2)}) async-start(s32[32,96,1]{1,2,0:T(1,128)} %bitcast.39), calls=%async_computation.1 | async-start | bytes 32768 | tf_op jit(solution)/shard_map/all_to_all | solution.py:119
  71.1 18.8 %copy-start.19 = (f32[512]{0:T(512)}, f32[512]{0:T(512)S(1)}, u32[]{:S(2)}) copy-start(f32[512]{0:T(512)S(1)} %add_rsqrt_fusion.2) | copy-start | bytes 6148
  81.4 3.4 copy-start.22
  89.9 6.7 copy-start.20
  89.9 6.7 copy-start.21
  89.9 8.6 %copy-start.15 = (pred[512]{0:T(512)(128)(4,1)S(1)}, pred[512]{0:T(512)(128)(4,1)}, u32[]{:S(2)}) copy-start(pred[512]{0:T(512)(128)(4,1)} %copy-done.14) | copy-start | bytes 1540
  108.5 1.0 copy-start.6
  119.2 37.4 %copy-start.9 = (bf16[1,1,1024,64]{2,3,1,0:T(8,128)(2,1)}, bf16[1,1,1024,64]{2,3,1,0:T(8,128)(2,1)S(1)}, u32[]{:S(2)}) copy-start(bf16[1,1,1024,64]{2,3,1,0:T(8,128)(2,1)S(1)} %scatter.9) | copy-start | bytes 393220
  156.6 21.7 %copy-start.18 = (bf16[2048]{0:T(1024)(128)(2,1)S(1)}, bf16[2048]{0:T(1024)(128)(2,1)}, u32[]{:S(2)}) copy-start(bf16[2048]{0:T(1024)(128)(2,1)} %param.40) | copy-start | bytes 12292
  156.6 21.7 %copy-start.7 = (bf16[1,1,1024,512]{3,2,1,0:T(8,128)(2,1)S(1)}, bf16[1,1,1024,512]{3,2,1,0:T(8,128)(2,1)}, u32[]{:S(2)}) copy-start(bf16[1,1,1024,512]{3,2,1,0:T(8,128)(2,1)} %copy-done.6) | copy-start | bytes 3145732
  222.1 1.3 copy-start.8
  222.1 1.9 copy-start.11
  223.9 16.0 %copy-start.2 = (bf16[512,2048]{1,0:T(8,128)(2,1)}, bf16[512,2048]{1,0:T(8,128)(2,1)S(1)}, u32[]{:S(2)}) copy-start(bf16[512,2048]{1,0:T(8,128)(2,1)S(1)} %fusion.15) | copy-start | bytes 6291460
  239.9 178.2 %all-to-all-start = ((bf16[32,96,2048]{2,1,0:T(8,128)(2,1)}), bf16[32,96,2048]{2,1,0:T(8,128)(2,1)}, u32[]{:S(2)}, u32[]{:S(2)}) async-start(bf16[32,96,2048]{2,1,0:T(8,128)(2,1)} %bitcast.147), calls=%async_computation | async-start | bytes 25165824 | tf_op jit(solution)/shard_map/all_to_all | solution.py:118
  578.7 4.2 copy-start.5
  578.7 4.4 copy-start.12
  578.7 4.8 copy-start.3
  578.7 4.8 copy-start.10
  578.7 175.4 %all-to-all-start.2 = ((bf16[32,96,2048]{2,1,0:T(8,128)(2,1)}), bf16[32,96,2048]{2,1,0:T(8,128)(2,1)}, u32[]{:S(2)}, u32[]{:S(2)}) async-start(bf16[32,96,2048]{2,1,0:T(8,128)(2,1)} %bitcast.148), calls=%async_computation.2 | async-start | bytes 25165824 | tf_op jit(solution)/shard_map/all_to_all | solution.py:124
  584.3 25.1 %copy-start.13 = (s32[3072]{0:T(1024)S(1)}, s32[3072]{0:T(1024)}, u32[]{:S(2)}) copy-start(s32[3072]{0:T(1024)} %get-tuple-element.99) | copy-start | bytes 36868
  806.2 19.3 %copy-start.16 = (pred[512]{0:T(512)(128)(4,1)S(1)}, pred[512]{0:T(512)(128)(4,1)}, u32[]{:S(2)}) copy-start(pred[512]{0:T(512)(128)(4,1)} %copy-done.14) | copy-start | bytes 1540
  825.5 25.4 %copy-start.1 = (bf16[512,16,128]{2,1,0:T(8,128)(2,1)S(1)}, bf16[512,16,128]{2,1,0:T(8,128)(2,1)}, u32[]{:S(2)}) copy-start(bf16[512,16,128]{2,1,0:T(8,128)(2,1)} %param.37) | copy-start | bytes 6291460
where the time goes:
time: 866 us; the launch traced here: 851 us
  waiting for transfers between devices  267 us (31%)
  local copies, waits for them, and re-layouts  201 us (23%)
  matrix products  157 us (18%)
  other arithmetic  133 us (15%)
  Pallas kernels  73.2 us (8%)
  starting transfers between devices  18.4 us (2%)
    all_to_all x1, waiting for transfers between devices, device_step(): recv_rows = lax.all_to_all(send_rows, 'dpa', 0, 0, tiled=True)  135 us
    all_to_all x1, waiting for transfers between devices, device_step(): back_rows = lax.all_to_all(expert_rows, 'dpa', 0, 0, tiled=True)  132 us
    another operation x3, Pallas kernels  71.6 us
    dot_general x1, matrix products, attention_block(): jnp.einsum('rbchk,khv->brchv', out_lat, w_uv, preferred_element_type=jnp....  35.7 us
    gather x1, local copies, waits for them, and re-layouts, device_step(): expert_rows = sorted_out[jnp.argsort(order)]  30 us
    gather x1, local copies, waits for them, and re-layouts, device_step(): recv_rows[order]  30 us
    gather x1, local copies, waits for them, and re-layouts, device_step(): pair_out = back_rows[slot].reshape(tokens, top_k, width)  30 us
    another operation x7, other arithmetic  28.6 us
  transfers between devices with their start and end apart: 3, of which 2 were waited for; matrix products, arithmetic and copies ran while one was open for 28% of the time, Pallas kernels for 0%

commit v1 on v0

v1 whole, which is shorter than its diff:
```python
import functools

import jax
import jax.numpy as jnp
from jax import lax
from jax.experimental import pallas as pl
from jax.experimental.pallas import tpu as pltpu
from jax.sharding import PartitionSpec as P

EPS = 1e-6
THETA = 10000.0
UNIT = 16
STAGES = 2
TILE = 256
BIG = 60000000


def rms_norm(vals, gain):
    vals_f32 = vals.astype(jnp.float32)
    inv_rms = lax.rsqrt(jnp.mean(vals_f32 * vals_f32, axis=-1, keepdims=True) + EPS)
    return (vals_f32 * inv_rms * gain.astype(jnp.float32)).astype(jnp.bfloat16)


def nn_dot(lhs, rhs):
    return jnp.dot(lhs, rhs, preferred_element_type=jnp.float32)


def params(vmem=BIG):
    return pltpu.CompilerParams(vmem_limit_bytes=vmem)


def attn_kernel(ctx_ref, q_ref, uk_ref, uv_ref, lat_ref, kr_ref, cos_ref, sin_ref, out_ref, lat_t_ref, *, scale, nope):
    @pl.when(pl.program_id(0) == 0)
    def _():
        lat_t_ref[...] = lat_ref[...].T

    chunk = q_ref.shape[2]
    half = cos_ref.shape[0]
    block = min(TILE, chunk)
    for r in range(chunk // block):
        cols = slice(r * block, (r + 1) * block)
        q_lat = nn_dot(uk_ref[...], q_ref[0, :nope, cols]).astype(jnp.bfloat16)
        first = q_ref[0, nope:nope + half, cols].astype(jnp.float32)
        second = q_ref[0, nope + half:, cols].astype(jnp.float32)
        cos_tab, sin_tab = cos_ref[:, cols], sin_ref[:, cols]
        q_rope = jnp.concatenate([first * cos_tab - second * sin_tab, second * cos_tab + first * sin_tab], axis=0).astype(jnp.bfloat16)
        scores = (nn_dot(lat_ref[...], q_lat) + nn_dot(kr_ref[...], q_rope)) * scale
        row_pos = lax.broadcasted_iota(jnp.int32, scores.shape, 1) + (ctx_ref[0] + r * block)
        key_pos = lax.broadcasted_iota(jnp.int32, scores.shape, 0)
        scores = jnp.where(key_pos <= row_pos, scores, -1e30)
        expo = jnp.exp(scores - jnp.max(scores, axis=0, keepdims=True))
        prob = (expo * (1.0 / jnp.sum(expo, axis=0, keepdims=True))).astype(jnp.bfloat16)
        out_lat = nn_dot(lat_t_ref[...], prob).astype(jnp.bfloat16)
        out_ref[0, :, cols] = lax.dot_general(uv_ref[...], out_lat, (((0,), (0,)), ((), ())), preferred_element_type=jnp.float32).astype(jnp.bfloat16)


def attention(ctx, q_t, w_uk, w_uv, lat, kr, cos_t, sin_t, scale, nope):
    heads, qdim, chunk = q_t.shape
    keys, rank = lat.shape
    vdim = w_uv.shape[1] // heads
    rope = kr.shape[1]
    full = lambda arr: pl.BlockSpec(arr.shape, lambda h, c: (0, 0))
    head = lambda rows, cols: pl.BlockSpec((1, rows, cols), lambda h, c: (h, 0, 0))
    spec = pltpu.PrefetchScalarGridSpec(
        num_scalar_prefetch=1, grid=(heads,),
        in_specs=[head(qdim, chunk), pl.BlockSpec((rank, nope), lambda h, c: (0, h)), pl.BlockSpec((rank, vdim), lambda h, c: (0, h)),
                  full(lat), full(kr), full(cos_t), full(sin_t)],
        out_specs=head(vdim, chunk), scratch_shapes=[pltpu.VMEM((rank, keys), jnp.bfloat16)])
    flops = 2 * heads * chunk * (rank * (nope + vdim) + keys * (2 * rank + rope))
    return pl.pallas_call(
        functools.partial(attn_kernel, scale=scale, nope=nope), grid_spec=spec,
        out_shape=jax.ShapeDtypeStruct((heads, vdim, chunk), jnp.bfloat16), compiler_params=params(),
        cost_estimate=pl.CostEstimate(flops=flops, bytes_accessed=16 * 2**20, transcendentals=heads * chunk * keys),
        name='attend')(ctx, q_t, w_uk, w_uv, lat, kr, cos_t, sin_t)


def send_kernel(pos_ref, u_ref, out_ref, *, base, top_k):
    tile = out_ref.shape[0]
    tokens = u_ref.shape[0]
    slots = lax.broadcasted_iota(jnp.int32, (tile, tokens), 0) + (base + pl.program_id(0) * tile)
    hit = slots == pos_ref[0:1, :]
    for i in range(1, top_k):
        hit = hit | (slots == pos_ref[i:i + 1, :])
    pick = jnp.where(hit, 1.0, 0.0).astype(jnp.bfloat16)
    out_ref[...] = nn_dot(pick, u_ref[...]).astype(jnp.bfloat16)


def send_rows(pos_t, normed, slots, base, top_k):
    tokens, width = normed.shape
    tile = min(TILE, slots)
    return pl.pallas_call(
        functools.partial(send_kernel, base=base, top_k=top_k), grid=(slots // tile,),
        in_specs=[pl.BlockSpec(pos_t.shape, lambda k: (0, 0)), pl.BlockSpec((tokens, width), lambda k: (0, 0))],
        out_specs=pl.BlockSpec((tile, width), lambda k: (k, 0)),
        out_shape=jax.ShapeDtypeStruct((slots, width), jnp.bfloat16), compiler_params=params(),
        cost_estimate=pl.CostEstimate(flops=2 * slots * tokens * width, bytes_accessed=slots * width * 2, transcendentals=0),
        name='pack_rows')(pos_t, normed)


def expert_kernel(counts_ref, in_ref, gate_hbm, up_hbm, down_hbm, rows_ref, gate_v, up_v, down_v, x_v, y_v, ids, lows, highs, w_sem, in_sem, out_sem, *, first, part, capacity, sources):
    per_tile = x_v.shape[1] // UNIT
    per_source = part // UNIT
    total_units = sources * per_source
    stride = total_units + per_tile
    local_exp = 2

    def weights(e):
        return [pltpu.make_async_copy(src.at[e], dst.at[e], w_sem.at[e]) for src, dst in ((gate_hbm, gate_v), (up_hbm, up_v), (down_hbm, down_v))]

    for e in range(local_exp):
        for copy in weights(e):
            copy.start()

    def list_units(e):
        def step(source, count):
            filled = counts_ref[source, e]
            for j in range(per_source):
                start = first + j * UNIT
                low = 0 if e == 0 else capacity - filled - start
                high = filled - start if e == 0 else UNIT
                ids[e * stride + count] = source * per_source + j
                lows[e * stride + count] = low
                highs[e * stride + count] = high
                need = filled > start if e == 0 else capacity - filled < start + UNIT
                count = count + need.astype(jnp.int32)
            return count
        return lax.fori_loop(0, sources, step, jnp.int32(0))

    units0, units1 = list_units(0), list_units(1)
    tiles0 = lax.div(units0 + (per_tile - 1), per_tile)
    tiles = tiles0 + lax.div(units1 + (per_tile - 1), per_tile)

    def place(t):
        e = jnp.where(t >= tiles0, 1, 0)
        begin = (t - jnp.where(t >= tiles0, tiles0, 0)) * per_tile
        size = jnp.minimum(per_tile, jnp.where(t >= tiles0, units1, units0) - begin)
        return e, e * stride + begin, size

    def in_copy(t, i):
        where = ids[place(t)[1] + i]
        return pltpu.make_async_copy(rows_ref.at[pl.ds(pl.multiple_of(where * UNIT, UNIT), UNIT), :], x_v.at[t % 2, pl.ds(pl.multiple_of(i * UNIT, UNIT), UNIT), :], in_sem.at[t % 2])

    def out_copy(t, i):
        where = ids[place(t)[1] + i]
        return pltpu.make_async_copy(y_v.at[t % 2, pl.ds(pl.multiple_of(i * UNIT, UNIT), UNIT), :], rows_ref.at[pl.ds(pl.multiple_of(where * UNIT, UNIT), UNIT), :], out_sem.at[t % 2])

    def each(t, copy_of, wait):
        @pl.loop(0, place(t)[2])
        def _(i):
            copy = copy_of(t, i)
            copy.wait() if wait else copy.start()

    for copy in weights(0):
        copy.wait()

    @pl.loop(0, tiles)
    def _(t):
        switch = t == tiles0

        @pl.when(switch)
        def _():
            for copy in weights(1):
                copy.wait()

        @pl.when(switch & (t > 0))
        def _():
            each(t - 1, out_copy, True)

        @pl.when(switch | (t == 0))
        def _():
            each(t, in_copy, False)

        each(t, in_copy, True)

        @pl.when((t + 1 < tiles) & (t + 1 != tiles0))
        def _():
            each(t + 1, in_copy, False)

        e, begin, _ = place(t)
        slot = t % 2
        rows = x_v[slot]
        gate = nn_dot(rows, gate_v[e])
        up = nn_dot(rows, up_v[e])
        act = (jax.nn.silu(gate) * up).astype(jnp.bfloat16)
        res = nn_dot(act, down_v[e])
        for i in range(per_tile):
            span = slice(i * UNIT, (i + 1) * UNIT)
            line = lax.broadcasted_iota(jnp.int32, (UNIT, rows.shape[1]), 0)
            mine = (line >= lows[begin + i]) & (line < highs[begin + i])
            y_v[slot, span, :] = jnp.where(mine, res[span], rows[span].astype(jnp.float32)).astype(jnp.bfloat16)

        @pl.when((t > 0) & jnp.logical_not(switch))
        def _():
            each(t - 1, out_copy, True)

        each(t, out_copy, False)

    @pl.when(tiles == tiles0)
    def _():
        for copy in weights(1):
            copy.wait()

    @pl.when(tiles > 0)
    def _():
        each(tiles - 1, out_copy, True)


def expert_rows(counts, rows, w_gate, w_up, w_down, first, part, capacity):
    slots, width = rows.shape
    sources = counts.shape[0]
    local_exp, _, ff = w_gate.shape
    tile = min(TILE, slots)
    room = local_exp * (slots // UNIT + tile // UNIT)
    anywhere = pl.BlockSpec(memory_space=pl.ANY)
    return pl.pallas_call(
        functools.partial(expert_kernel, first=first, part=part, capacity=capacity, sources=sources),
        in_specs=[pl.BlockSpec(memory_space=pltpu.SMEM)] + [anywhere] * 4, out_specs=anywhere,
        out_shape=jax.ShapeDtypeStruct((slots, width), jnp.bfloat16), input_output_aliases={1: 0},
        scratch_shapes=[pltpu.VMEM(w_gate.shape, jnp.bfloat16), pltpu.VMEM(w_up.shape, jnp.bfloat16), pltpu.VMEM(w_down.shape, jnp.bfloat16),
                        pltpu.VMEM((2, tile, width), jnp.bfloat16), pltpu.VMEM((2, tile, width), jnp.bfloat16),
                        pltpu.SMEM((room,), jnp.int32), pltpu.SMEM((room,), jnp.int32), pltpu.SMEM((room,), jnp.int32),
                        pltpu.SemaphoreType.DMA((local_exp,)), pltpu.SemaphoreType.DMA((2,)), pltpu.SemaphoreType.DMA((2,))],
        compiler_params=params(),
        cost_estimate=pl.CostEstimate(flops=6 * slots * width * ff, bytes_accessed=12 * width * ff, transcendentals=0),
        name='expert_rows')(counts, rows, w_gate, w_up, w_down)


def merge_kernel(pos_ref, gate_ref, keep_ref, start_ref, rows_ref, out_ref, acc_ref, *, base, top_k, last):
    k = pl.program_id(0)

    @pl.when(k == 0)
    def _():
        acc_ref[...] = start_ref[...]

    tile = rows_ref.shape[0]
    tokens = acc_ref.shape[0]
    slots = lax.broadcasted_iota(jnp.int32, (tokens, tile), 1) + (base + k * tile)
    mix = jnp.zeros((tokens, tile), jnp.float32)
    for i in range(top_k):
        mix = jnp.where(slots == pos_ref[:, i:i + 1], gate_ref[:, i:i + 1], mix)
    high = mix.astype(jnp.bfloat16)
    rest = mix - high.astype(jnp.float32)
    mid = rest.astype(jnp.bfloat16)
    low = (rest - mid.astype(jnp.float32)).astype(jnp.bfloat16)
    rows = rows_ref[...]
    acc_ref[...] += nn_dot(high, rows) + (nn_dot(mid, rows) + nn_dot(low, rows))

    @pl.when(k == pl.num_programs(0) - 1)
    def _():
        if last:
            out_ref[...] = jnp.where(keep_ref[:, 0:1] > 0, acc_ref[...], 0.0).astype(out_ref.dtype)
        else:
            out_ref[...] = acc_ref[...]


def merge_rows(pos, gates, keep, start, rows, base, top_k, last):
    slots, width = rows.shape
    tokens = start.shape[0]
    tile = min(TILE, slots)
    full = lambda arr: pl.BlockSpec(arr.shape, lambda k: (0, 0))
    return pl.pallas_call(
        functools.partial(merge_kernel, base=base, top_k=top_k, last=last), grid=(slots // tile,),
        in_specs=[full(pos), full(gates), full(keep), full(start), pl.BlockSpec((tile, width), lambda k: (k, 0))],
        out_specs=pl.BlockSpec((tokens, width), lambda k: (0, 0)),
        out_shape=jax.ShapeDtypeStruct((tokens, width), jnp.bfloat16 if last else jnp.float32),
        scratch_shapes=[pltpu.VMEM((tokens, width), jnp.float32)], compiler_params=params(),
        cost_estimate=pl.CostEstimate(flops=6 * slots * tokens * width, bytes_accessed=slots * width * 2, transcendentals=0),
        name='merge_rows')(pos, gates, keep, start, rows)


def solution(mesh):
    group = mesh.shape['dpa']
    tok_spec = P(('dp', 'dpa'))
    whole = P()
    exp_spec = P('dpa')

    def device_step(x_in, chunk_len, ctx_len, lat_cache, rope_cache, topk_idx, g_attn, w_q, w_dkv, g_kv, w_kr, w_uk, w_uv, w_o, g_ffn, w_router, w_sh_gate, w_sh_up, w_sh_down, w_exp_gate, w_exp_up, w_exp_down):
        tokens, width = x_in.shape[2], x_in.shape[3]
        top_k = topk_idx.shape[-1]
        local_exp = w_exp_gate.shape[0]
        experts = group * local_exp
        capacity = tokens * top_k // group
        part = capacity // STAGES
        slots = group * part
        length = chunk_len[0, 0]
        ctx = ctx_len[0, 0]

        row_ids = jnp.arange(tokens, dtype=jnp.int32)
        valid = row_ids < length
        choice = topk_idx.reshape(tokens, top_k)
        picked = (choice[:, :, None] == jnp.arange(experts, dtype=jnp.int32)) & valid[:, None, None]
        member = jnp.any(picked, axis=1)
        before = (row_ids[:, None] > row_ids[None, :]).astype(jnp.bfloat16)
        rank_in = nn_dot(before, member.astype(jnp.bfloat16)).astype(jnp.int32)
        counts = jnp.sum(member.astype(jnp.int32), axis=0)
        counts_in = lax.all_to_all(counts.reshape(group, local_exp), 'dpa', 0, 0, tiled=True)
        ids = jnp.arange(experts, dtype=jnp.int32)
        place = jnp.where(ids % local_exp == 0, rank_in, capacity - 1 - rank_in)
        pos_all = (place // part) * slots + (ids // local_exp) * part + place % part
        pos = jnp.sum(jnp.where(picked, pos_all[:, None, :], 0), axis=2)
        pos = jnp.where(valid[:, None], pos, -1)
        pad_k = (-top_k) % 8
        pos = jnp.pad(pos, ((0, 0), (0, pad_k)), constant_values=-1)
        pos_t = pos.T

        chunk_x = x_in.reshape(tokens, width)
        normed_x = rms_norm(chunk_x, g_attn)
        rope_dim = w_kr.shape[1]
        heads, qdim = w_q.shape[1], w_q.shape[2]
        nope_dim = qdim - rope_dim
        half = rope_dim // 2
        q_t = jnp.einsum('cd,dhq->hqc', normed_x, w_q, preferred_element_type=jnp.float32).astype(jnp.bfloat16)
        inv_freq = THETA ** (-2.0 * jnp.arange(half, dtype=jnp.float32) / (2 * half))
        angle = (ctx + row_ids).astype(jnp.float32)[:, None] * inv_freq
        cos_tab, sin_tab = jnp.cos(angle), jnp.sin(angle)
        lat_new = rms_norm(nn_dot(normed_x, w_dkv), g_kv)
        kr_raw = nn_dot(normed_x, w_kr)
        kr_new = jnp.concatenate([kr_raw[:, :half] * cos_tab - kr_raw[:, half:] * sin_tab, kr_raw[:, half:] * cos_tab + kr_raw[:, :half] * sin_tab], axis=1).astype(jnp.bfloat16)

        def write_window(cache, new_rows):
            old_rows = lax.dynamic_slice_in_dim(cache, ctx, tokens, axis=0)
            return lax.dynamic_update_slice_in_dim(cache, jnp.where(valid[:, None], new_rows, old_rows), ctx, axis=0)

        lat_upd = write_window(lat_cache[0, 0], lat_new)
        rope_upd = write_window(rope_cache[0, 0], kr_new)
        out_head = attention(ctx_len.reshape(1), q_t, w_uk.reshape(w_uk.shape[0], -1), w_uv.reshape(w_uv.shape[0], -1), lat_upd, rope_upd, cos_tab.T, sin_tab.T, qdim ** -0.5, nope_dim)
        attn_out = jnp.einsum('hvc,hvd->cd', out_head, w_o, preferred_element_type=jnp.float32).astype(jnp.bfloat16)
        hidden = (chunk_x.astype(jnp.float32) + attn_out.astype(jnp.float32)).astype(jnp.bfloat16)
        normed = rms_norm(hidden, g_ffn)

        packed = [send_rows(pos_t, normed, slots, h * slots, top_k).reshape(group, part, width) for h in range(STAGES)]
        shared_act = (jax.nn.silu(nn_dot(normed, w_sh_gate)) * nn_dot(normed, w_sh_up)).astype(jnp.bfloat16)
        packed[1], shared_act = lax.optimization_barrier((packed[1], shared_act))
        landed = [lax.all_to_all(rows, 'dpa', 0, 0, tiled=True) for rows in packed]
        total = hidden.astype(jnp.float32) + nn_dot(shared_act, w_sh_down)
        route_prob = jax.nn.softmax(nn_dot(normed, w_router), axis=-1)
        gates = jnp.sum(jnp.where(picked, route_prob[:, None, :], 0.0), axis=2)
        gates = jnp.pad(gates, ((0, 0), (0, pad_k)))
        keep = jnp.broadcast_to(valid.astype(jnp.int32)[:, None], (tokens, 8))

        returned = []
        for h in range(STAGES):
            done = expert_rows(counts_in, landed[h].reshape(slots, width), w_exp_gate, w_exp_up, w_exp_down, h * part, part, capacity)
            returned.append(lax.all_to_all(done.reshape(group, part, width), 'dpa', 0, 0, tiled=True))
        for h in range(STAGES):
            total = merge_rows(pos, gates, keep, total, returned[h].reshape(slots, width), h * slots, top_k, h == STAGES - 1)
        return total.reshape(x_in.shape), lat_upd.reshape(lat_cache.shape), rope_upd.reshape(rope_cache.shape)

    return jax.shard_map(device_step, mesh=mesh, in_specs=(tok_spec,) * 6 + (whole,) * 13 + (exp_spec,) * 3, out_specs=(tok_spec, tok_spec, tok_spec), check_vma=False)
```

time: 866 us -> 530 us (0.61)
  local copies, waits for them, and re-layouts: 201 us -> 22.9 us
  Pallas kernels: 73.2 us -> 222 us
  other arithmetic: 133 us -> 15.6 us
  matrix products: 157 us -> 55.7 us
  waiting for transfers between devices: 267 us -> 176 us
    pallas_call x0 -> x7, Pallas kernels: none -> 222 us  [the longest x2 95.4 us: expert_rows(): pl.pallas_call(functools.partial(expert_kernel, first=first, part=part, c...]
    gather x9 -> x0, local copies, waits for them, and re-layouts: 149 us -> none  [the longest x1 30 us: device_step(): expert_rows = sorted_out[jnp.argsort(order)]]
    all_to_all x3 -> x5, waiting for transfers between devices: 267 us -> 176 us  [the longest x2 93.4 us: device_step(): landed = [lax.all_to_all(rows, 'dpa', 0, 0, tiled=True) for rows in packed]]
    dot_general x9 -> x8, matrix products: 130 us -> 45.4 us  [the longest x7 36.4 us: nn_dot(): return jnp.dot(lhs, rhs, preferred_element_type=jnp.float32)]
    another operation x3 -> x0, Pallas kernels: 71.6 us -> none
    convert_element_type x5 -> x3, other arithmetic: 34.5 us -> 2.68 us  [the longest x1 2.09 us: device_step(): jnp.einsum('cd,dhq->hqc', normed_x, w_q, preferred_element_type=jnp.float32)]
    another operation x7 -> x1, other arithmetic: 28.6 us -> 1.86 us
    scatter-add x1 -> x0, other arithmetic: 22.3 us -> none  [device_step(): jnp.bincount(recv_key, length=local_exp + 1)[:local_exp].astype(jnp.int32)]
  transfers between devices with their start and end apart: 3 -> 5, of which waited for: 2 -> 4; matrix products, arithmetic and copies ran while one was open for 28% -> 17% of each run, Pallas kernels for 0% -> 38%
where the time goes in v1:
time: 530 us; the launch traced here: 522 us
  Pallas kernels  222 us (42%)
  waiting for transfers between devices  176 us (33%)
  matrix products  55.7 us (11%)
  starting transfers between devices  26.6 us (5%)
  local copies, waits for them, and re-layouts  22.9 us (4%)
  other arithmetic  15.6 us (3%)
    pallas_call x2, Pallas kernels, expert_rows(): pl.pallas_call(functools.partial(expert_kernel, first=first, part=part, c...  95.4 us
    all_to_all x2, waiting for transfers between devices, device_step(): landed = [lax.all_to_all(rows, 'dpa', 0, 0, tiled=True) for rows in packed]  93.4 us
    all_to_all x2, waiting for transfers between devices, device_step(): lax.all_to_all(done.reshape(group, part, width), 'dpa', 0, 0, tiled=True)  82.2 us
    pallas_call x1, Pallas kernels, attention(): pl.pallas_call(functools.partial(attn_kernel, scale=scale, nope=nope), gr...  65.5 us
    pallas_call x2, Pallas kernels, merge_rows(): pl.pallas_call(functools.partial(merge_kernel, base=base, top_k=top_k, la...  44.9 us
    dot_general x7, matrix products, nn_dot(): return jnp.dot(lhs, rhs, preferred_element_type=jnp.float32)  36.4 us
    pallas_call x2, Pallas kernels, send_rows(): pl.pallas_call(functools.partial(send_kernel, base=base, top_k=top_k), gr...  16.5 us
    all_to_all x2, starting transfers between devices, device_step(): landed = [lax.all_to_all(rows, 'dpa', 0, 0, tiled=True) for rows in packed]  10.9 us
  transfers between devices with their start and end apart: 5, of which 4 were waited for; matrix products, arithmetic and copies ran while one was open for 17% of the time, Pallas kernels for 38%

profile of v1, /device:TPU:103, one launch (start us, length us, event | category | flops | bytes accessed | tf_op | source)
XLA Modules:
  0.0 521.5 jit_solution(7820354868277418314)
XLA Ops:
  0.7 1.4 copy.120
  2.7 0.7 copy.112
  3.7 0.7 all_to_all.19
  4.4 8.0 %all-to-all-start = ((s32[32,1,2]{2,1,0:T(1,128)}), s32[32,1,2]{2,1,0:T(1,128)}, u32[]{:S(2)}, u32[]{:S(2)}) async-start(s32[32,1,2]{2,1,0:T(1,128)} %bitcast.15), calls=%async_computation | async-start | bytes 32768 | tf_op jit(solution)/shard_map/all_to_all | solution.py:296
  14.2 1.3 convert_element_type.78
  15.5 2.1 fusion.3
  18.1 0.6 convert_element_type.74
  19.3 0.8 copy.90
  21.1 0.8 broadcast_select_fusion
  21.9 1.6 multiply_sine_fusion.1
  23.6 2.4 fusion.27
  26.0 1.9 fusion.15
  27.8 0.8 pad_bitcast_fusion
  28.6 0.7 copy.97.pos_ref
  29.3 3.9 multiply_reduce_fusion
  33.2 1.6 copy.89
  34.8 10.2 %fusion.31 = f32[512,3072]{0,1:S(1)} fusion(bf16[2048,3072]{0,1:T(8,128)(2,1)} %bitcast.85, bf16[1,1,512,2048]{3,2,1,0:T(8,128)(2,1)} %param.22, f32[2048]{0:T(1024)S(1)} %copy-done.19, f32[512]{0:T(512)S(1)} %copy-done.23), kind=kOutput, calls=%fused_computation.74 | convolution fusion | flops 6446645248 | bytes 20981760
  45.1 2.1 convert_bitcast_fusion.q_ref
  47.4 0.7 dynamic_update_slice.7.kr_ref
  48.4 3.1 dynamic_update_slice.6.lat_ref
  51.4 6.8 %copy_bitcast_fusion = (bf16[512,2048]{1,0:T(8,128)(2,1)}, bf16[512,2048]{1,0:T(8,128)(2,1)}) fusion(bf16[64,8,16,128]{3,2,1,0:T(8,128)(2,1)} %bitcast.77, bf16[64,8,16,128]{3,2,1,0:T(8,128)(2,1)} %bitcast.78), kind=kLoop, calls=%fused_computation.16 | loop fusion | bytes 8388608 | tf_op jit(solution)/shard_map/reshape | solution.py:326
  58.2 65.5 %attend.1 = bf16[16,128,512]{2,1,0:T(8,128)(2,1)} custom-call(s32[1]{0:T(128)} %bitcast.67.ctx_ref, bf16[16,192,512]{2,1,0:T(8,128)(2,1)} %convert_bitcast_fusion.q_ref, bf16[512,2048]{1,0:T(8,128)(2,1)} %get-tuple-element.35.uk_ref, bf16[512,2048]{1,0:T(8,128)(2,1)} %get-tuple-element.34.uv_ref, bf16[1024,512]{1,0:T(8,128)(2,1)} %copy-done.3, ...), custom_call_target="tpu_custom_call" | custom-call | flops 20401094656 | bytes 16777216 | tf_op jit(solution)/shard_map/attend/pallas_call | solution.py:70
  123.7 9.0 %fusion = (f32[512]{0:T(512)S(1)}, bf16[512,2048]{1,0:T(8,128)(2,1)S(1)}) fusion(bf16[16,128,512]{2,1,0:T(8,128)(2,1)} %attend.1, bf16[16,128,2048]{2,1,0:T(8,128)(2,1)} %param.35, bf16[1,1,512,2048]{3,2,1,0:T(8,128)(2,1)S(1)} %copy-done.4), kind=kOutput, calls=%fused_computation.7 | convolution fusion | flops 4303355392 | bytes 14682112 | tf_op jit(solution)/shard_map/hvc,hvd->cd/dot_general | solution.py:327
  132.7 1.3 copy-done.5
  134.0 1.9 fusion.2.u_ref
  135.9 8.2 %pack_rows.3 = bf16[1536,2048]{1,0:T(8,128)(2,1)} custom-call(s32[8,512]{1,0:T(8,128)} %copy.97.pos_ref, bf16[512,2048]{1,0:T(8,128)(2,1)} %fusion.2.u_ref), custom_call_target="tpu_custom_call" | custom-call | flops 3221225472 | bytes 6291456 | tf_op jit(solution)/shard_map/pack_rows/pallas_call | solution.py:91
  144.1 7.1 %all-to-all-start.1 = ((bf16[32,48,2048]{2,1,0:T(8,128)(2,1)}), bf16[32,48,2048]{2,1,0:T(8,128)(2,1)}, u32[]{:S(2)}, u32[]{:S(2)}) async-start(bf16[32,48,2048]{2,1,0:T(8,128)(2,1)} %bitcast.73), calls=%async_computation.1 | async-start | bytes 12582912 | tf_op jit(solution)/shard_map/all_to_all | solution.py:334
  151.2 8.3 %pack_rows.2 = bf16[1536,2048]{1,0:T(8,128)(2,1)} custom-call(s32[8,512]{1,0:T(8,128)} %copy.97.pos_ref, bf16[512,2048]{1,0:T(8,128)(2,1)} %fusion.2.u_ref), custom_call_target="tpu_custom_call" | custom-call | flops 3221225472 | bytes 6291456 | tf_op jit(solution)/shard_map/pack_rows/pallas_call | solution.py:91
  159.6 9.6 %fusion.34 = f32[512,2816]{1,0:T(8,128)S(1)} fusion(bf16[512,2048]{1,0:T(8,128)(2,1)S(1)} %copy-done.2, bf16[2048,2816]{1,0:T(8,128)(2,1)} %param.38), kind=kOutput, calls=%fused_computation.76 | convolution fusion | flops 5905580032 | bytes 19398656 | tf_op jit(solution)/shard_map/dot_general | solution.py:25
  169.2 7.9 %multiply_convert_fusion = bf16[512,2816]{1,0:T(8,128)(2,1)} fusion(f32[512,2816]{1,0:T(8,128)S(1)} %fusion.34, bf16[512,2048]{1,0:T(8,128)(2,1)S(1)} %copy-done.2, bf16[2048,2816]{1,0:T(8,128)(2,1)S(1)} %bitcast.87), kind=kOutput, calls=%fused_computation.6 | convolution fusion | flops 5914230784 | bytes 22282240 | tf_op jit(solution)/shard_map/dot_general | solution.py:25
  177.1 58.7 %all-to-all-done.1 = bf16[32,48,2048]{2,1,0:T(8,128)(2,1)} async-done(((bf16[32,48,2048]{2,1,0:T(8,128)(2,1)}), bf16[32,48,2048]{2,1,0:T(8,128)(2,1)}, u32[]{:S(2)}, u32[]{:S(2)}) %all-to-all-start.1) | async-done | bytes 6291488 | tf_op jit(solution)/shard_map/all_to_all | solution.py:334
  235.8 3.8 all-to-all-start.3
  239.6 0.8 copy.99
  240.4 0.7 copy.101.counts_ref
  241.1 47.6 %expert_rows.2 = bf16[1536,2048]{1,0:T(8,128)(2,1)} custom-call(s32[32,2]{1,0:T(8,128)} %copy.101.counts_ref, bf16[1536,2048]{1,0:T(8,128)(2,1)} %bitcast.18.in_ref, bf16[2,2048,1408]{2,1,0:T(8,128)(2,1)} %gate_hbm.3, bf16[2,2048,1408]{2,1,0:T(8,128)(2,1)} %up_hbm.3, bf16[2,1408,2048]{2,1,0:T(8,128)(2,1)} %down_hbm.3), custom_call_target="tpu_custom_call", output_to_operand_aliasing={{}: (1, {})} | custom-call | flops 26575110144 | bytes 34603008 | tf_op jit(solution)/shard_map/expert_rows/pallas_call | solution.py:215
  288.7 34.7 %all-to-all-done.3 = bf16[32,48,2048]{2,1,0:T(8,128)(2,1)} async-done(((bf16[32,48,2048]{2,1,0:T(8,128)(2,1)}), bf16[32,48,2048]{2,1,0:T(8,128)(2,1)}, u32[]{:S(2)}, u32[]{:S(2)}) %all-to-all-start.3) | async-done | bytes 6291488 | tf_op jit(solution)/shard_map/all_to_all | solution.py:334
  323.5 3.8 all-to-all-start.2
  327.3 47.7 %expert_rows.3 = bf16[1536,2048]{1,0:T(8,128)(2,1)} custom-call(s32[32,2]{1,0:T(8,128)} %copy.101.counts_ref, bf16[1536,2048]{1,0:T(8,128)(2,1)} %bitcast.21.in_ref, bf16[2,2048,1408]{2,1,0:T(8,128)(2,1)} %gate_hbm.3, bf16[2,2048,1408]{2,1,0:T(8,128)(2,1)} %up_hbm.3, bf16[2,1408,2048]{2,1,0:T(8,128)(2,1)} %down_hbm.3), custom_call_target="tpu_custom_call", output_to_operand_aliasing={{}: (1, {})} | custom-call | flops 26575110144 | bytes 34603008 | tf_op jit(solution)/shard_map/expert_rows/pallas_call | solution.py:215
  375.0 36.2 %all-to-all-done.2 = bf16[32,48,2048]{2,1,0:T(8,128)(2,1)} async-done(((bf16[32,48,2048]{2,1,0:T(8,128)(2,1)}), bf16[32,48,2048]{2,1,0:T(8,128)(2,1)}, u32[]{:S(2)}, u32[]{:S(2)}) %all-to-all-start.2) | async-done | bytes 6291488 | tf_op jit(solution)/shard_map/all_to_all | solution.py:344
  411.2 3.9 all-to-all-start.4
  415.2 0.8 copy.103
  416.0 0.8 fusion.33
  417.2 0.7 pad.9.gate_ref
  417.9 11.4 %convert_add_fusion.1.start_ref = f32[512,2048]{1,0:T(8,128)} fusion(bf16[512,2048]{1,0:T(8,128)(2,1)} %copy-done.5, bf16[512,2816]{1,0:T(8,128)(2,1)} %multiply_convert_fusion, bf16[2816,2048]{1,0:T(8,128)(2,1)} %param.40), kind=kOutput, calls=%fused_computation.3 | convolution fusion | flops 5907677184 | bytes 20709376 | tf_op jit(solution)/shard_map/dot_general | solution.py:25
  429.4 0.8 broadcast_in_dim.91.keep_ref
  430.2 22.7 %merge_rows.2.start_ref = f32[512,2048]{1,0:T(8,128)} custom-call(s32[512,8]{1,0:T(8,128)} %get-tuple-element.25.pos_ref, f32[512,8]{1,0:T(8,128)} %pad.9.gate_ref, s32[512,8]{1,0:T(8,128)} %broadcast_in_dim.91.keep_ref, f32[512,2048]{1,0:T(8,128)} %convert_add_fusion.1.start_ref, bf16[1536,2048]{1,0:T(8,128)(2,1)} %bitcast.20.rows_ref), custom_call_target="tpu_custom_call" | custom-call | flops 9663676416 | bytes 6291456 | tf_op jit(solution)/shard_map/merge_rows/pallas_call | solution.py:261
  452.9 46.0 %all-to-all-done.4 = bf16[32,48,2048]{2,1,0:T(8,128)(2,1)} async-done(((bf16[32,48,2048]{2,1,0:T(8,128)(2,1)}), bf16[32,48,2048]{2,1,0:T(8,128)(2,1)}, u32[]{:S(2)}, u32[]{:S(2)}) %all-to-all-start.4) | async-done | bytes 6291488 | tf_op jit(solution)/shard_map/all_to_all | solution.py:344
  498.9 22.2 %merge_rows.3 = bf16[512,2048]{1,0:T(8,128)(2,1)} custom-call(s32[512,8]{1,0:T(8,128)} %get-tuple-element.25.pos_ref, f32[512,8]{1,0:T(8,128)} %pad.9.gate_ref, s32[512,8]{1,0:T(8,128)} %broadcast_in_dim.91.keep_ref, f32[512,2048]{1,0:T(8,128)} %merge_rows.2.start_ref, bf16[1536,2048]{1,0:T(8,128)(2,1)} %bitcast.23.rows_ref), custom_call_target="tpu_custom_call" | custom-call | flops 9663676416 | bytes 6291456 | tf_op jit(solution)/shard_map/merge_rows/pallas_call | solution.py:261
  (80 shorter events, 4.4 us)
Async XLA Ops:
  0.6 28.6 %copy-start = (bf16[2048,512]{1,0:T(8,128)(2,1)S(1)}, bf16[2048,512]{1,0:T(8,128)(2,1)}, u32[]{:S(2)}) copy-start(bf16[2048,512]{1,0:T(8,128)(2,1)} %param.30) | copy-start | bytes 6291460
  0.6 18.6 %copy-start.11 = (bf16[1,1,1024,64]{2,3,1,0:T(8,128)(2,1)S(1)}, bf16[1,1,1024,64]{2,3,1,0:T(8,128)(2,1)}, u32[]{:S(2)}) copy-start(bf16[1,1,1024,64]{2,3,1,0:T(8,128)(2,1)} %param.26) | copy-start | bytes 393220
  0.7 17.4 %copy-start.21 = (bf16[2048]{0:T(1024)(128)(2,1)S(1)}, bf16[2048]{0:T(1024)(128)(2,1)}, u32[]{:S(2)}) copy-start(bf16[2048]{0:T(1024)(128)(2,1)} %param.28) | copy-start | bytes 12292
  0.7 18.0 %copy-start.22 = (bf16[2048]{0:T(1024)(128)(2,1)S(1)}, bf16[2048]{0:T(1024)(128)(2,1)}, u32[]{:S(2)}) copy-start(bf16[2048]{0:T(1024)(128)(2,1)} %param.36) | copy-start | bytes 12292
  2.7 18.0 %copy-start.17 = (pred[512]{0:T(512)(128)(4,1)}, pred[512]{0:T(512)(128)(4,1)S(1)}, u32[]{:S(2)}) copy-start(pred[512]{0:T(512)(128)(4,1)S(1)} %iota_compare_fusion.7) | copy-start | bytes 1540
  3.4 17.3 %copy-start.12 = (s32[1,1,512,6]{2,3,1,0:T(8,128)}, s32[1,1,512,6]{2,3,1,0:T(8,128)S(1)}, u32[]{:S(2)}) copy-start(s32[1,1,512,6]{2,3,1,0:T(8,128)S(1)} %copy.112) | copy-start | bytes 36868
  4.4 139.7 %all-to-all-start = ((s32[32,1,2]{2,1,0:T(1,128)}), s32[32,1,2]{2,1,0:T(1,128)}, u32[]{:S(2)}, u32[]{:S(2)}) async-start(s32[32,1,2]{2,1,0:T(1,128)} %bitcast.15), calls=%async_computation | async-start | bytes 32768 | tf_op jit(solution)/shard_map/all_to_all | solution.py:296
  21.1 4.8 copy-start.16
  21.1 4.8 copy-start.24
  21.1 8.2 %copy-start.19 = (f32[2048]{0:T(1024)S(1)}, f32[2048]{0:T(1024)}, u32[]{:S(2)}) copy-start(f32[2048]{0:T(1024)} %convert_element_type.74) | copy-start | bytes 24580
  21.1 8.1 %copy-start.23 = (f32[512]{0:T(512)S(1)}, f32[512]{0:T(512)}, u32[]{:S(2)}) copy-start(f32[512]{0:T(512)} %add_rsqrt_fusion.2) | copy-start | bytes 6148
  45.1 2.2 copy-start.9
  45.1 2.1 copy-start.10
  45.1 2.1 copy-start.18
  45.1 2.3 copy-start.6
  45.1 3.0 copy-start.20
  48.1 10.1 %copy-start.7 = (bf16[1024,64]{1,0:T(8,128)(2,1)}, bf16[1024,64]{1,0:T(8,128)(2,1)S(1)}, u32[]{:S(2)}) copy-start(bf16[1024,64]{1,0:T(8,128)(2,1)S(1)} %dynamic_update_slice.7.kr_ref) | copy-start | bytes 393220
  51.4 6.8 %copy-start.3 = (bf16[1024,512]{1,0:T(8,128)(2,1)}, bf16[1024,512]{1,0:T(8,128)(2,1)S(1)}, u32[]{:S(2)}) copy-start(bf16[1024,512]{1,0:T(8,128)(2,1)S(1)} %dynamic_update_slice.6.lat_ref) | copy-start | bytes 3145732
  58.2 65.5 %copy-start.4 = (bf16[1,1,512,2048]{3,2,1,0:T(8,128)(2,1)S(1)}, bf16[1,1,512,2048]{3,2,1,0:T(8,128)(2,1)}, u32[]{:S(2)}) copy-start(bf16[1,1,512,2048]{3,2,1,0:T(8,128)(2,1)} %param.22) | copy-start | bytes 6291460
  123.7 10.4 %copy-start.15 = (f32[2048]{0:T(1024)S(1)}, f32[2048]{0:T(1024)}, u32[]{:S(2)}) copy-start(f32[2048]{0:T(1024)} %convert_element_type.85) | copy-start | bytes 24580
  132.7 1.3 copy-start.5
  144.1 91.7 %all-to-all-start.1 = ((bf16[32,48,2048]{2,1,0:T(8,128)(2,1)}), bf16[32,48,2048]{2,1,0:T(8,128)(2,1)}, u32[]{:S(2)}, u32[]{:S(2)}) async-start(bf16[32,48,2048]{2,1,0:T(8,128)(2,1)} %bitcast.73), calls=%async_computation.1 | async-start | bytes 12582912 | tf_op jit(solution)/shard_map/all_to_all | solution.py:334
  151.2 8.4 %copy-start.2 = (bf16[512,2048]{1,0:T(8,128)(2,1)S(1)}, bf16[512,2048]{1,0:T(8,128)(2,1)}, u32[]{:S(2)}) copy-start(bf16[512,2048]{1,0:T(8,128)(2,1)} %fusion.2.u_ref) | copy-start | bytes 6291460
  151.2 18.0 %slice-start = ((s8[11534336]{0:T(1024)(128)(4,1)}), s8[3145728]{0:T(1024)(128)(4,1)S(1)}, s32[]{:S(2)}) async-start(s8[11534336]{0:T(1024)(128)(4,1)} %bitcast.86), calls=%async_computation.5 | async-start | bytes 6291456
  159.6 9.7 %slice-start.1 = ((s8[11534336]{0:T(1024)(128)(4,1)}), s8[4194304]{0:T(1024)(128)(4,1)S(1)}, s32[]{:S(2)}) async-start(s8[11534336]{0:T(1024)(128)(4,1)} %bitcast.86), calls=%async_computation.6 | async-start | bytes 8388608
  159.6 9.7 %slice-start.2 = ((s8[11534336]{0:T(1024)(128)(4,1)}), s8[4194304]{0:T(1024)(128)(4,1)S(1)}, s32[]{:S(2)}) async-start(s8[11534336]{0:T(1024)(128)(4,1)} %bitcast.86), calls=%async_computation.7 | async-start | bytes 8388608
  235.8 87.7 %all-to-all-start.3 = ((bf16[32,48,2048]{2,1,0:T(8,128)(2,1)}), bf16[32,48,2048]{2,1,0:T(8,128)(2,1)}, u32[]{:S(2)}, u32[]{:S(2)}) async-start(bf16[32,48,2048]{2,1,0:T(8,128)(2,1)} %bitcast.72), calls=%async_computation.3 | async-start | bytes 12582912 | tf_op jit(solution)/shard_map/all_to_all | solution.py:334
  323.5 87.7 %all-to-all-start.2 = ((bf16[32,48,2048]{2,1,0:T(8,128)(2,1)}), bf16[32,48,2048]{2,1,0:T(8,128)(2,1)}, u32[]{:S(2)}, u32[]{:S(2)}) async-start(bf16[32,48,2048]{2,1,0:T(8,128)(2,1)} %bitcast.19), calls=%async_computation.2 | async-start | bytes 12582912 | tf_op jit(solution)/shard_map/all_to_all | solution.py:344
  411.2 4.0 copy-start.8
  411.2 4.8 copy-start.14
  411.2 5.6 %copy-start.13 = (s32[1,1,512,6]{2,3,1,0:T(8,128)S(1)}, s32[1,1,512,6]{2,3,1,0:T(8,128)}, u32[]{:S(2)}) copy-start(s32[1,1,512,6]{2,3,1,0:T(8,128)} %copy-done.12) | copy-start | bytes 36868
  411.2 87.7 %all-to-all-start.4 = ((bf16[32,48,2048]{2,1,0:T(8,128)(2,1)}), bf16[32,48,2048]{2,1,0:T(8,128)(2,1)}, u32[]{:S(2)}, u32[]{:S(2)}) async-start(bf16[32,48,2048]{2,1,0:T(8,128)(2,1)} %bitcast.22), calls=%async_computation.4 | async-start | bytes 12582912 | tf_op jit(solution)/shard_map/all_to_all | solution.py:344
  498.9 22.2 %copy-start.1 = (bf16[2048,512]{1,0:T(8,128)(2,1)S(1)}, bf16[2048,512]{1,0:T(8,128)(2,1)}, u32[]{:S(2)}) copy-start(bf16[2048,512]{1,0:T(8,128)(2,1)} %param.30) | copy-start | bytes 6291460

commit v2 on v1

--- a/solution.py
+++ b/solution.py
@@ -11,7 +11,11 @@
 THETA = 10000.0
 UNIT = 16
 STAGES = 2
+LANES = 128
 TILE = 256
+HEADS_STEP = 2
+PACK_TILE = 768
+MERGE_TILE = 768
 BIG = 60000000
 
 
@@ -35,23 +39,44 @@
         lat_t_ref[...] = lat_ref[...].T
 
     chunk = q_ref.shape[2]
+    keys = lat_ref.shape[0]
     half = cos_ref.shape[0]
     block = min(TILE, chunk)
-    for r in range(chunk // block):
+    chains = [(g, r) for g in range(q_ref.shape[0]) for r in range(chunk // block)]
+
+    def seen(r):
+        return keys - chunk + (r + 1) * block
+
+    def scores_of(g, r):
         cols = slice(r * block, (r + 1) * block)
-        q_lat = nn_dot(uk_ref[...], q_ref[0, :nope, cols]).astype(jnp.bfloat16)
-        first = q_ref[0, nope:nope + half, cols].astype(jnp.float32)
-        second = q_ref[0, nope + half:, cols].astype(jnp.float32)
+        q_lat = nn_dot(uk_ref[:, g * nope:(g + 1) * nope], q_ref[g, :nope, cols]).astype(jnp.bfloat16)
+        first = q_ref[g, nope:nope + half, cols].astype(jnp.float32)
+        second = q_ref[g, nope + half:, cols].astype(jnp.float32)
         cos_tab, sin_tab = cos_ref[:, cols], sin_ref[:, cols]
         q_rope = jnp.concatenate([first * cos_tab - second * sin_tab, second * cos_tab + first * sin_tab], axis=0).astype(jnp.bfloat16)
-        scores = (nn_dot(lat_ref[...], q_lat) + nn_dot(kr_ref[...], q_rope)) * scale
-        row_pos = lax.broadcasted_iota(jnp.int32, scores.shape, 1) + (ctx_ref[0] + r * block)
+        return nn_dot(lat_ref[:seen(r), :], q_lat) + nn_dot(kr_ref[:seen(r), :], q_rope)
+
+    def prob_of(scores, r):
+        scores = scores * scale
+        row_pos = lax.broadcasted_iota(jnp.int32, (1, block), 1) + (ctx_ref[0] + r * block)
         key_pos = lax.broadcasted_iota(jnp.int32, scores.shape, 0)
         scores = jnp.where(key_pos <= row_pos, scores, -1e30)
         expo = jnp.exp(scores - jnp.max(scores, axis=0, keepdims=True))
-        prob = (expo * (1.0 / jnp.sum(expo, axis=0, keepdims=True))).astype(jnp.bfloat16)
-        out_lat = nn_dot(lat_t_ref[...], prob).astype(jnp.bfloat16)
-        out_ref[0, :, cols] = lax.dot_general(uv_ref[...], out_lat, (((0,), (0,)), ((), ())), preferred_element_type=jnp.float32).astype(jnp.bfloat16)
+        return (expo * (1.0 / jnp.sum(expo, axis=0, keepdims=True))).astype(jnp.bfloat16)
+
+    def finish(prob, g, r):
+        vdim = out_ref.shape[1]
+        out_lat = nn_dot(lat_t_ref[:, :seen(r)], prob).astype(jnp.bfloat16)
+        out_ref[g, :, r * block:(r + 1) * block] = lax.dot_general(uv_ref[:, g * vdim:(g + 1) * vdim], out_lat, (((0,), (0,)), ((), ())), preferred_element_type=jnp.float32).astype(jnp.bfloat16)
+
+    scores, probs = {0: scores_of(*chains[0])}, {}
+    for i, (g, r) in enumerate(chains):
+        if i + 1 < len(chains):
+            scores[i + 1] = scores_of(*chains[i + 1])
+        probs[i] = prob_of(scores.pop(i), r)
+        if i > 0:
+            finish(probs.pop(i - 1), *chains[i - 1])
+    finish(probs.pop(len(chains) - 1), *chains[-1])
 
 
 def attention(ctx, q_t, w_uk, w_uv, lat, kr, cos_t, sin_t, scale, nope):
@@ -60,10 +85,10 @@
     vdim = w_uv.shape[1] // heads
     rope = kr.shape[1]
     full = lambda arr: pl.BlockSpec(arr.shape, lambda h, c: (0, 0))
-    head = lambda rows, cols: pl.BlockSpec((1, rows, cols), lambda h, c: (h, 0, 0))
+    head = lambda rows, cols: pl.BlockSpec((HEADS_STEP, rows, cols), lambda h, c: (h, 0, 0))
     spec = pltpu.PrefetchScalarGridSpec(
-        num_scalar_prefetch=1, grid=(heads,),
-        in_specs=[head(qdim, chunk), pl.BlockSpec((rank, nope), lambda h, c: (0, h)), pl.BlockSpec((rank, vdim), lambda h, c: (0, h)),
+        num_scalar_prefetch=1, grid=(heads // HEADS_STEP,),
+        in_specs=[head(qdim, chunk), pl.BlockSpec((rank, HEADS_STEP * nope), lambda h, c: (0, h)), pl.BlockSpec((rank, HEADS_STEP * vdim), lambda h, c: (0, h)),
                   full(lat), full(kr), full(cos_t), full(sin_t)],
         out_specs=head(vdim, chunk), scratch_shapes=[pltpu.VMEM((rank, keys), jnp.bfloat16)])
     flops = 2 * heads * chunk * (rank * (nope + vdim) + keys * (2 * rank + rope))
@@ -87,7 +112,7 @@
 
 def send_rows(pos_t, normed, slots, base, top_k):
     tokens, width = normed.shape
-    tile = min(TILE, slots)
+    tile = min(PACK_TILE, slots)
     return pl.pallas_call(
         functools.partial(send_kernel, base=base, top_k=top_k), grid=(slots // tile,),
         in_specs=[pl.BlockSpec(pos_t.shape, lambda k: (0, 0)), pl.BlockSpec((tokens, width), lambda k: (0, 0))],
@@ -225,7 +250,7 @@
         name='expert_rows')(counts, rows, w_gate, w_up, w_down)
 
 
-def merge_kernel(pos_ref, gate_ref, keep_ref, start_ref, rows_ref, out_ref, acc_ref, *, base, top_k, last):
+def merge_kernel(pos_ref, gate_ref, keep_ref, start_ref, rows_ref, out_ref, acc_ref, mix_ref, *, base, top_k, last):
     k = pl.program_id(0)
 
     @pl.when(k == 0)
@@ -234,16 +259,26 @@
 
     tile = rows_ref.shape[0]
     tokens = acc_ref.shape[0]
-    slots = lax.broadcasted_iota(jnp.int32, (tokens, tile), 1) + (base + k * tile)
-    mix = jnp.zeros((tokens, tile), jnp.float32)
-    for i in range(top_k):
-        mix = jnp.where(slots == pos_ref[:, i:i + 1], gate_ref[:, i:i + 1], mix)
-    high = mix.astype(jnp.bfloat16)
-    rest = mix - high.astype(jnp.float32)
-    mid = rest.astype(jnp.bfloat16)
-    low = (rest - mid.astype(jnp.float32)).astype(jnp.bfloat16)
-    rows = rows_ref[...]
-    acc_ref[...] += nn_dot(high, rows) + (nn_dot(mid, rows) + nn_dot(low, rows))
+    strip = 32
+    for t in range(0, tokens, strip):
+        at = slice(t, t + strip)
+        spots = [jnp.broadcast_to(pos_ref[at, i:i + 1], (strip, LANES)) for i in range(top_k)]
+        gates = [jnp.broadcast_to(gate_ref[at, i:i + 1], (strip, LANES)) for i in range(top_k)]
+        for c in range(0, tile, LANES):
+            slots = lax.broadcasted_iota(jnp.int32, (strip, LANES), 1) + (base + c + k * tile)
+            mix = jnp.zeros((strip, LANES), jnp.float32)
+            for i in range(top_k):
+                mix = jnp.where(slots == spots[i], gates[i], mix)
+            high = mix.astype(jnp.bfloat16)
+            rest = mix - high.astype(jnp.float32)
+            mid = rest.astype(jnp.bfloat16)
+            low = (rest - mid.astype(jnp.float32)).astype(jnp.bfloat16)
+            for n, piece in enumerate((high, mid, low)):
+                mix_ref[n * tokens + t:n * tokens + t + strip, c:c + LANES] = piece
+    width = acc_ref.shape[1]
+    for j in range(0, width, TILE):
+        parts = nn_dot(mix_ref[...], rows_ref[:, j:j + TILE])
+        acc_ref[:, j:j + TILE] += parts[:tokens] + (parts[tokens:2 * tokens] + parts[2 * tokens:])
 
     @pl.when(k == pl.num_programs(0) - 1)
     def _():
@@ -256,14 +291,14 @@
 def merge_rows(pos, gates, keep, start, rows, base, top_k, last):
     slots, width = rows.shape
     tokens = start.shape[0]
-    tile = min(TILE, slots)
+    tile = min(MERGE_TILE, slots)
     full = lambda arr: pl.BlockSpec(arr.shape, lambda k: (0, 0))
     return pl.pallas_call(
         functools.partial(merge_kernel, base=base, top_k=top_k, last=last), grid=(slots // tile,),
         in_specs=[full(pos), full(gates), full(keep), full(start), pl.BlockSpec((tile, width), lambda k: (k, 0))],
         out_specs=pl.BlockSpec((tokens, width), lambda k: (0, 0)),
         out_shape=jax.ShapeDtypeStruct((tokens, width), jnp.bfloat16 if last else jnp.float32),
-        scratch_shapes=[pltpu.VMEM((tokens, width), jnp.float32)], compiler_params=params(),
+        scratch_shapes=[pltpu.VMEM((tokens, width), jnp.float32), pltpu.VMEM((3 * tokens, tile), jnp.bfloat16)], compiler_params=params(),
         cost_estimate=pl.CostEstimate(flops=6 * slots * tokens * width, bytes_accessed=slots * width * 2, transcendentals=0),
         name='merge_rows')(pos, gates, keep, start, rows)
 

time: 530 us -> 508 us (0.958)
  Pallas kernels: 222 us -> 184 us
  starting transfers between devices: 26.6 us -> 36.8 us
  waiting for transfers between devices: 176 us -> 182 us
    pallas_call x1, Pallas kernels: 65.5 us -> 35.5 us  [attention(): pl.pallas_call(functools.partial(attn_kernel, scale=scale, nope=nope), gr...]
    all_to_all x2, starting transfers between devices: 10.9 us -> 20.8 us  [device_step(): landed = [lax.all_to_all(rows, 'dpa', 0, 0, tiled=True) for rows in packed]]
    pallas_call x2, Pallas kernels: 44.9 us -> 37.2 us  [merge_rows(): pl.pallas_call(functools.partial(merge_kernel, base=base, top_k=top_k, la...]
    all_to_all x2, waiting for transfers between devices: 82.2 us -> 87.5 us  [device_step(): lax.all_to_all(done.reshape(group, part, width), 'dpa', 0, 0, tiled=True)]
  transfers between devices with their start and end apart: 5 -> 5, of which waited for: 4 -> 4; matrix products, arithmetic and copies ran while one was open for 17% -> 18% of each run, Pallas kernels for 38% -> 33%
where the time goes in v2:
time: 508 us; the launch traced here: 500 us
  Pallas kernels  184 us (36%)
  waiting for transfers between devices  182 us (36%)
  matrix products  55.7 us (11%)
  starting transfers between devices  36.8 us (7%)
  local copies, waits for them, and re-layouts  23.1 us (5%)
  other arithmetic  15.6 us (3%)
    pallas_call x2, Pallas kernels, expert_rows(): pl.pallas_call(functools.partial(expert_kernel, first=first, part=part, c...  94.9 us
    all_to_all x2, waiting for transfers between devices, device_step(): landed = [lax.all_to_all(rows, 'dpa', 0, 0, tiled=True) for rows in packed]  94.2 us
    all_to_all x2, waiting for transfers between devices, device_step(): lax.all_to_all(done.reshape(group, part, width), 'dpa', 0, 0, tiled=True)  87.5 us
    pallas_call x2, Pallas kernels, merge_rows(): pl.pallas_call(functools.partial(merge_kernel, base=base, top_k=top_k, la...  37.2 us
    dot_general x7, matrix products, nn_dot(): return jnp.dot(lhs, rhs, preferred_element_type=jnp.float32)  36.4 us
    pallas_call x1, Pallas kernels, attention(): pl.pallas_call(functools.partial(attn_kernel, scale=scale, nope=nope), gr...  35.5 us
    all_to_all x2, starting transfers between devices, device_step(): landed = [lax.all_to_all(rows, 'dpa', 0, 0, tiled=True) for rows in packed]  20.8 us
    pallas_call x2, Pallas kernels, send_rows(): pl.pallas_call(functools.partial(send_kernel, base=base, top_k=top_k), gr...  16.3 us
  transfers between devices with their start and end apart: 5, of which 4 were waited for; matrix products, arithmetic and copies ran while one was open for 18% of the time, Pallas kernels for 33%

profile of v2, /device:TPU:103, one launch (start us, length us, event | category | flops | bytes accessed | tf_op | source)
XLA Modules:
  0.0 499.7 jit_solution(17657305635424730547)
XLA Ops:
  0.7 1.4 copy.120
  2.7 0.7 copy.112
  3.7 0.7 all_to_all.19
  4.4 8.0 %all-to-all-start = ((s32[32,1,2]{2,1,0:T(1,128)}), s32[32,1,2]{2,1,0:T(1,128)}, u32[]{:S(2)}, u32[]{:S(2)}) async-start(s32[32,1,2]{2,1,0:T(1,128)} %bitcast.15), calls=%async_computation | async-start | bytes 32768 | tf_op jit(solution)/shard_map/all_to_all | solution.py:331
  14.2 1.3 convert_element_type.78
  15.5 2.1 fusion.3
  18.1 0.6 convert_element_type.74
  19.3 0.8 copy.90
  21.1 0.8 broadcast_select_fusion
  21.9 1.6 multiply_sine_fusion.1
  23.6 2.4 fusion.27
  25.9 1.9 fusion.15
  27.8 0.8 pad_bitcast_fusion
  28.6 0.7 copy.97.pos_ref
  29.3 3.9 multiply_reduce_fusion
  33.2 1.6 copy.89
  34.8 10.2 %fusion.31 = f32[512,3072]{0,1:S(1)} fusion(bf16[2048,3072]{0,1:T(8,128)(2,1)} %bitcast.85, bf16[1,1,512,2048]{3,2,1,0:T(8,128)(2,1)} %param.22, f32[2048]{0:T(1024)S(1)} %copy-done.19, f32[512]{0:T(512)S(1)} %copy-done.23), kind=kOutput, calls=%fused_computation.74 | convolution fusion | flops 6446645248 | bytes 20981760
  45.1 2.1 convert_bitcast_fusion.q_ref
  47.4 0.8 dynamic_update_slice.7.kr_ref
  48.5 3.1 dynamic_update_slice.6.lat_ref
  51.6 6.8 %copy_bitcast_fusion = (bf16[512,2048]{1,0:T(8,128)(2,1)}, bf16[512,2048]{1,0:T(8,128)(2,1)}) fusion(bf16[64,8,16,128]{3,2,1,0:T(8,128)(2,1)} %bitcast.77, bf16[64,8,16,128]{3,2,1,0:T(8,128)(2,1)} %bitcast.78), kind=kLoop, calls=%fused_computation.16 | loop fusion | bytes 8388608 | tf_op jit(solution)/shard_map/reshape | solution.py:361
  58.4 35.5 %attend.1 = bf16[16,128,512]{2,1,0:T(8,128)(2,1)} custom-call(s32[1]{0:T(128)} %bitcast.67.ctx_ref, bf16[16,192,512]{2,1,0:T(8,128)(2,1)} %convert_bitcast_fusion.q_ref, bf16[512,2048]{1,0:T(8,128)(2,1)} %get-tuple-element.35.uk_ref, bf16[512,2048]{1,0:T(8,128)(2,1)} %get-tuple-element.34.uv_ref, bf16[1024,512]{1,0:T(8,128)(2,1)} %copy-done.3, ...), custom_call_target="tpu_custom_call" | custom-call | flops 20401094656 | bytes 16777216 | tf_op jit(solution)/shard_map/attend/pallas_call | solution.py:95
  93.8 9.0 %fusion = (f32[512]{0:T(512)S(1)}, bf16[512,2048]{1,0:T(8,128)(2,1)S(1)}) fusion(bf16[16,128,512]{2,1,0:T(8,128)(2,1)} %attend.1, bf16[16,128,2048]{2,1,0:T(8,128)(2,1)} %param.35, bf16[1,1,512,2048]{3,2,1,0:T(8,128)(2,1)S(1)} %copy-done.4), kind=kOutput, calls=%fused_computation.7 | convolution fusion | flops 4303355392 | bytes 14682112 | tf_op jit(solution)/shard_map/hvc,hvd->cd/dot_general | solution.py:362
  102.9 1.3 copy-done.5
  104.2 1.9 fusion.2.u_ref
  106.1 8.1 %pack_rows.3 = bf16[1536,2048]{1,0:T(8,128)(2,1)} custom-call(s32[8,512]{1,0:T(8,128)} %copy.97.pos_ref, bf16[512,2048]{1,0:T(8,128)(2,1)} %fusion.2.u_ref), custom_call_target="tpu_custom_call" | custom-call | flops 3221225472 | bytes 6291456 | tf_op jit(solution)/shard_map/pack_rows/pallas_call | solution.py:116
  114.1 17.0 %all-to-all-start.1 = ((bf16[32,48,2048]{2,1,0:T(8,128)(2,1)}), bf16[32,48,2048]{2,1,0:T(8,128)(2,1)}, u32[]{:S(2)}, u32[]{:S(2)}) async-start(bf16[32,48,2048]{2,1,0:T(8,128)(2,1)} %bitcast.73), calls=%async_computation.1 | async-start | bytes 12582912 | tf_op jit(solution)/shard_map/all_to_all | solution.py:369
  131.1 8.3 %pack_rows.2 = bf16[1536,2048]{1,0:T(8,128)(2,1)} custom-call(s32[8,512]{1,0:T(8,128)} %copy.97.pos_ref, bf16[512,2048]{1,0:T(8,128)(2,1)} %fusion.2.u_ref), custom_call_target="tpu_custom_call" | custom-call | flops 3221225472 | bytes 6291456 | tf_op jit(solution)/shard_map/pack_rows/pallas_call | solution.py:116
  139.4 9.6 %fusion.34 = f32[512,2816]{1,0:T(8,128)S(1)} fusion(bf16[512,2048]{1,0:T(8,128)(2,1)S(1)} %copy-done.2, bf16[2048,2816]{1,0:T(8,128)(2,1)} %param.38), kind=kOutput, calls=%fused_computation.76 | convolution fusion | flops 5905580032 | bytes 19398656 | tf_op jit(solution)/shard_map/dot_general | solution.py:29
  149.1 7.9 %multiply_convert_fusion = bf16[512,2816]{1,0:T(8,128)(2,1)} fusion(f32[512,2816]{1,0:T(8,128)S(1)} %fusion.34, bf16[512,2048]{1,0:T(8,128)(2,1)S(1)} %copy-done.2, bf16[2048,2816]{1,0:T(8,128)(2,1)S(1)} %bitcast.87), kind=kOutput, calls=%fused_computation.6 | convolution fusion | flops 5914230784 | bytes 22282240 | tf_op jit(solution)/shard_map/dot_general | solution.py:29
  157.0 58.8 %all-to-all-done.1 = bf16[32,48,2048]{2,1,0:T(8,128)(2,1)} async-done(((bf16[32,48,2048]{2,1,0:T(8,128)(2,1)}), bf16[32,48,2048]{2,1,0:T(8,128)(2,1)}, u32[]{:S(2)}, u32[]{:S(2)}) %all-to-all-start.1) | async-done | bytes 6291488 | tf_op jit(solution)/shard_map/all_to_all | solution.py:369
  215.7 3.8 all-to-all-start.3
  219.6 0.8 copy.99
  220.4 0.7 copy.101.counts_ref
  221.1 47.4 %expert_rows.2 = bf16[1536,2048]{1,0:T(8,128)(2,1)} custom-call(s32[32,2]{1,0:T(8,128)} %copy.101.counts_ref, bf16[1536,2048]{1,0:T(8,128)(2,1)} %bitcast.18.in_ref, bf16[2,2048,1408]{2,1,0:T(8,128)(2,1)} %gate_hbm.3, bf16[2,2048,1408]{2,1,0:T(8,128)(2,1)} %up_hbm.3, bf16[2,1408,2048]{2,1,0:T(8,128)(2,1)} %down_hbm.3), custom_call_target="tpu_custom_call", output_to_operand_aliasing={{}: (1, {})} | custom-call | flops 26575110144 | bytes 34603008 | tf_op jit(solution)/shard_map/expert_rows/pallas_call | solution.py:240
  268.5 35.5 %all-to-all-done.3 = bf16[32,48,2048]{2,1,0:T(8,128)(2,1)} async-done(((bf16[32,48,2048]{2,1,0:T(8,128)(2,1)}), bf16[32,48,2048]{2,1,0:T(8,128)(2,1)}, u32[]{:S(2)}, u32[]{:S(2)}) %all-to-all-start.3) | async-done | bytes 6291488 | tf_op jit(solution)/shard_map/all_to_all | solution.py:369
  303.9 4.0 all-to-all-start.2
  308.0 47.5 %expert_rows.3 = bf16[1536,2048]{1,0:T(8,128)(2,1)} custom-call(s32[32,2]{1,0:T(8,128)} %copy.101.counts_ref, bf16[1536,2048]{1,0:T(8,128)(2,1)} %bitcast.21.in_ref, bf16[2,2048,1408]{2,1,0:T(8,128)(2,1)} %gate_hbm.3, bf16[2,2048,1408]{2,1,0:T(8,128)(2,1)} %up_hbm.3, bf16[2,1408,2048]{2,1,0:T(8,128)(2,1)} %down_hbm.3), custom_call_target="tpu_custom_call", output_to_operand_aliasing={{}: (1, {})} | custom-call | flops 26575110144 | bytes 34603008 | tf_op jit(solution)/shard_map/expert_rows/pallas_call | solution.py:240
  355.4 36.9 %all-to-all-done.2 = bf16[32,48,2048]{2,1,0:T(8,128)(2,1)} async-done(((bf16[32,48,2048]{2,1,0:T(8,128)(2,1)}), bf16[32,48,2048]{2,1,0:T(8,128)(2,1)}, u32[]{:S(2)}, u32[]{:S(2)}) %all-to-all-start.2) | async-done | bytes 6291488 | tf_op jit(solution)/shard_map/all_to_all | solution.py:379
  392.4 4.0 all-to-all-start.4
  396.4 0.8 copy.103
  397.2 0.8 fusion.33
  398.4 0.7 pad.9.gate_ref
  399.2 11.4 %convert_add_fusion.1.start_ref = f32[512,2048]{1,0:T(8,128)} fusion(bf16[512,2048]{1,0:T(8,128)(2,1)} %copy-done.5, bf16[512,2816]{1,0:T(8,128)(2,1)} %multiply_convert_fusion, bf16[2816,2048]{1,0:T(8,128)(2,1)} %param.40), kind=kOutput, calls=%fused_computation.3 | convolution fusion | flops 5907677184 | bytes 20709376 | tf_op jit(solution)/shard_map/dot_general | solution.py:29
  410.6 0.8 broadcast_in_dim.91.keep_ref
  411.4 18.8 %merge_rows.2.start_ref = f32[512,2048]{1,0:T(8,128)} custom-call(s32[512,8]{1,0:T(8,128)} %get-tuple-element.25.pos_ref, f32[512,8]{1,0:T(8,128)} %pad.9.gate_ref, s32[512,8]{1,0:T(8,128)} %broadcast_in_dim.91.keep_ref, f32[512,2048]{1,0:T(8,128)} %convert_add_fusion.1.start_ref, bf16[1536,2048]{1,0:T(8,128)(2,1)} %bitcast.20.rows_ref), custom_call_target="tpu_custom_call" | custom-call | flops 9663676416 | bytes 6291456 | tf_op jit(solution)/shard_map/merge_rows/pallas_call | solution.py:296
  430.2 50.6 %all-to-all-done.4 = bf16[32,48,2048]{2,1,0:T(8,128)(2,1)} async-done(((bf16[32,48,2048]{2,1,0:T(8,128)(2,1)}), bf16[32,48,2048]{2,1,0:T(8,128)(2,1)}, u32[]{:S(2)}, u32[]{:S(2)}) %all-to-all-start.4) | async-done | bytes 6291488 | tf_op jit(solution)/shard_map/all_to_all | solution.py:379
  480.8 18.4 %merge_rows.3 = bf16[512,2048]{1,0:T(8,128)(2,1)} custom-call(s32[512,8]{1,0:T(8,128)} %get-tuple-element.25.pos_ref, f32[512,8]{1,0:T(8,128)} %pad.9.gate_ref, s32[512,8]{1,0:T(8,128)} %broadcast_in_dim.91.keep_ref, f32[512,2048]{1,0:T(8,128)} %merge_rows.2.start_ref, bf16[1536,2048]{1,0:T(8,128)(2,1)} %bitcast.23.rows_ref), custom_call_target="tpu_custom_call" | custom-call | flops 9663676416 | bytes 6291456 | tf_op jit(solution)/shard_map/merge_rows/pallas_call | solution.py:296
  (80 shorter events, 4.4 us)
Async XLA Ops:
  0.6 28.6 %copy-start = (bf16[2048,512]{1,0:T(8,128)(2,1)S(1)}, bf16[2048,512]{1,0:T(8,128)(2,1)}, u32[]{:S(2)}) copy-start(bf16[2048,512]{1,0:T(8,128)(2,1)} %param.30) | copy-start | bytes 6291460
  0.6 18.6 %copy-start.11 = (bf16[1,1,1024,64]{2,3,1,0:T(8,128)(2,1)S(1)}, bf16[1,1,1024,64]{2,3,1,0:T(8,128)(2,1)}, u32[]{:S(2)}) copy-start(bf16[1,1,1024,64]{2,3,1,0:T(8,128)(2,1)} %param.26) | copy-start | bytes 393220
  0.7 17.4 %copy-start.21 = (bf16[2048]{0:T(1024)(128)(2,1)S(1)}, bf16[2048]{0:T(1024)(128)(2,1)}, u32[]{:S(2)}) copy-start(bf16[2048]{0:T(1024)(128)(2,1)} %param.28) | copy-start | bytes 12292
  0.7 18.0 %copy-start.22 = (bf16[2048]{0:T(1024)(128)(2,1)S(1)}, bf16[2048]{0:T(1024)(128)(2,1)}, u32[]{:S(2)}) copy-start(bf16[2048]{0:T(1024)(128)(2,1)} %param.36) | copy-start | bytes 12292
  2.7 18.0 %copy-start.17 = (pred[512]{0:T(512)(128)(4,1)}, pred[512]{0:T(512)(128)(4,1)S(1)}, u32[]{:S(2)}) copy-start(pred[512]{0:T(512)(128)(4,1)S(1)} %iota_compare_fusion.7) | copy-start | bytes 1540
  3.4 17.3 %copy-start.12 = (s32[1,1,512,6]{2,3,1,0:T(8,128)}, s32[1,1,512,6]{2,3,1,0:T(8,128)S(1)}, u32[]{:S(2)}) copy-start(s32[1,1,512,6]{2,3,1,0:T(8,128)S(1)} %copy.112) | copy-start | bytes 36868
  4.4 109.8 %all-to-all-start = ((s32[32,1,2]{2,1,0:T(1,128)}), s32[32,1,2]{2,1,0:T(1,128)}, u32[]{:S(2)}, u32[]{:S(2)}) async-start(s32[32,1,2]{2,1,0:T(1,128)} %bitcast.15), calls=%async_computation | async-start | bytes 32768 | tf_op jit(solution)/shard_map/all_to_all | solution.py:331
  21.1 4.8 copy-start.16
  21.1 4.8 copy-start.24
  21.1 8.1 %copy-start.19 = (f32[2048]{0:T(1024)S(1)}, f32[2048]{0:T(1024)}, u32[]{:S(2)}) copy-start(f32[2048]{0:T(1024)} %convert_element_type.74) | copy-start | bytes 24580
  21.1 8.1 %copy-start.23 = (f32[512]{0:T(512)S(1)}, f32[512]{0:T(512)}, u32[]{:S(2)}) copy-start(f32[512]{0:T(512)} %add_rsqrt_fusion.2) | copy-start | bytes 6148
  45.0 2.2 copy-start.9
  45.1 2.1 copy-start.10
  45.1 2.1 copy-start.18
  45.1 2.3 copy-start.6
  45.1 3.1 copy-start.20
  48.2 10.1 %copy-start.7 = (bf16[1024,64]{1,0:T(8,128)(2,1)}, bf16[1024,64]{1,0:T(8,128)(2,1)S(1)}, u32[]{:S(2)}) copy-start(bf16[1024,64]{1,0:T(8,128)(2,1)S(1)} %dynamic_update_slice.7.kr_ref) | copy-start | bytes 393220
  51.6 6.8 %copy-start.3 = (bf16[1024,512]{1,0:T(8,128)(2,1)}, bf16[1024,512]{1,0:T(8,128)(2,1)S(1)}, u32[]{:S(2)}) copy-start(bf16[1024,512]{1,0:T(8,128)(2,1)S(1)} %dynamic_update_slice.6.lat_ref) | copy-start | bytes 3145732
  58.3 35.5 %copy-start.4 = (bf16[1,1,512,2048]{3,2,1,0:T(8,128)(2,1)S(1)}, bf16[1,1,512,2048]{3,2,1,0:T(8,128)(2,1)}, u32[]{:S(2)}) copy-start(bf16[1,1,512,2048]{3,2,1,0:T(8,128)(2,1)} %param.22) | copy-start | bytes 6291460
  93.8 10.4 %copy-start.15 = (f32[2048]{0:T(1024)S(1)}, f32[2048]{0:T(1024)}, u32[]{:S(2)}) copy-start(f32[2048]{0:T(1024)} %convert_element_type.85) | copy-start | bytes 24580
  102.9 1.3 copy-start.5
  114.1 101.6 %all-to-all-start.1 = ((bf16[32,48,2048]{2,1,0:T(8,128)(2,1)}), bf16[32,48,2048]{2,1,0:T(8,128)(2,1)}, u32[]{:S(2)}, u32[]{:S(2)}) async-start(bf16[32,48,2048]{2,1,0:T(8,128)(2,1)} %bitcast.73), calls=%async_computation.1 | async-start | bytes 12582912 | tf_op jit(solution)/shard_map/all_to_all | solution.py:369
  131.1 8.3 %copy-start.2 = (bf16[512,2048]{1,0:T(8,128)(2,1)S(1)}, bf16[512,2048]{1,0:T(8,128)(2,1)}, u32[]{:S(2)}) copy-start(bf16[512,2048]{1,0:T(8,128)(2,1)} %fusion.2.u_ref) | copy-start | bytes 6291460
  131.1 17.9 %slice-start = ((s8[11534336]{0:T(1024)(128)(4,1)}), s8[3145728]{0:T(1024)(128)(4,1)S(1)}, s32[]{:S(2)}) async-start(s8[11534336]{0:T(1024)(128)(4,1)} %bitcast.86), calls=%async_computation.5 | async-start | bytes 6291456
  139.4 9.7 %slice-start.1 = ((s8[11534336]{0:T(1024)(128)(4,1)}), s8[4194304]{0:T(1024)(128)(4,1)S(1)}, s32[]{:S(2)}) async-start(s8[11534336]{0:T(1024)(128)(4,1)} %bitcast.86), calls=%async_computation.6 | async-start | bytes 8388608
  139.4 9.7 %slice-start.2 = ((s8[11534336]{0:T(1024)(128)(4,1)}), s8[4194304]{0:T(1024)(128)(4,1)S(1)}, s32[]{:S(2)}) async-start(s8[11534336]{0:T(1024)(128)(4,1)} %bitcast.86), calls=%async_computation.7 | async-start | bytes 8388608
  215.7 88.2 %all-to-all-start.3 = ((bf16[32,48,2048]{2,1,0:T(8,128)(2,1)}), bf16[32,48,2048]{2,1,0:T(8,128)(2,1)}, u32[]{:S(2)}, u32[]{:S(2)}) async-start(bf16[32,48,2048]{2,1,0:T(8,128)(2,1)} %bitcast.72), calls=%async_computation.3 | async-start | bytes 12582912 | tf_op jit(solution)/shard_map/all_to_all | solution.py:369
  303.9 88.4 %all-to-all-start.2 = ((bf16[32,48,2048]{2,1,0:T(8,128)(2,1)}), bf16[32,48,2048]{2,1,0:T(8,128)(2,1)}, u32[]{:S(2)}, u32[]{:S(2)}) async-start(bf16[32,48,2048]{2,1,0:T(8,128)(2,1)} %bitcast.19), calls=%async_computation.2 | async-start | bytes 12582912 | tf_op jit(solution)/shard_map/all_to_all | solution.py:379
  392.4 4.0 copy-start.8
  392.4 4.8 copy-start.14
  392.4 5.7 %copy-start.13 = (s32[1,1,512,6]{2,3,1,0:T(8,128)S(1)}, s32[1,1,512,6]{2,3,1,0:T(8,128)}, u32[]{:S(2)}) copy-start(s32[1,1,512,6]{2,3,1,0:T(8,128)} %copy-done.12) | copy-start | bytes 36868
  392.4 88.4 %all-to-all-start.4 = ((bf16[32,48,2048]{2,1,0:T(8,128)(2,1)}), bf16[32,48,2048]{2,1,0:T(8,128)(2,1)}, u32[]{:S(2)}, u32[]{:S(2)}) async-start(bf16[32,48,2048]{2,1,0:T(8,128)(2,1)} %bitcast.22), calls=%async_computation.4 | async-start | bytes 12582912 | tf_op jit(solution)/shard_map/all_to_all | solution.py:379
  480.8 18.4 %copy-start.1 = (bf16[2048,512]{1,0:T(8,128)(2,1)S(1)}, bf16[2048,512]{1,0:T(8,128)(2,1)}, u32[]{:S(2)}) copy-start(bf16[2048,512]{1,0:T(8,128)(2,1)} %param.30) | copy-start | bytes 6291460
